TPU v7x, 128 devices: a whole 4x4x4 slice. The times are simulated.
128 devices in a mesh: row: 16 (over x, y_hi, core), col: 8 (over y_lo, z).
Axes of the slice: x: 4, y: 4 (y_hi: 2, y_lo: 2; y = y_hi * 2 + y_lo), z: 4, core: 2. Of those that a mesh axis runs over, the one named last changes fastest.
Arguments:
- out_grad: bfloat16 [1280, 8192], P('col', 'row'), may hold values from -32 to 32
- gate_act: bfloat16 [1280, 29568], P('row', 'col'), may hold values from -8 to 8
- up_act: bfloat16 [1280, 29568], P('row', 'col'), may hold values from -6 to 6
- gate_codes: int32 [29568, 4096], P('col', 'row'), may hold values from 0 to 255
- gate_scales: int32 [512, 29568], P('row', 'col'), may hold values from 40 to 71
- up_codes: int32 [29568, 4096], P('col', 'row'), may hold values from 0 to 255
- up_scales: int32 [512, 29568], P('row', 'col'), may hold values from 40 to 71
- down_codes: int32 [8192, 14784], P('row', 'col'), may hold values from 0 to 255
- down_scales: int32 [1848, 8192], P('col', 'row'), may hold values from 40 to 71
- tensor_scales: float32 [3], replicated, may hold values from 0.001 to 0.003
Outputs:
- grad_unit: bfloat16 [1280, 8192], P('col', 'row')
- grad_amax: float32 [1], replicated
All inputs are finite; a program needn't handle non-finite values. Where the computation divides by a largest or mean magnitude, that divisor is 1e-20 or more.
Results may differ from a plain program's by a relative error of at most 0.025.
Values may be sent and summed in bfloat16 or wider, within the bound.
No kernel may reach another device: no remote copies, remote signals or barrier semaphores. Data moves between devices by JAX's collectives and lax.ppermute only.
A program may use at most 128 MiB of HBM per device.

v0:
```python
import functools

import jax
import jax.numpy as jnp
from jax import lax
from jax.sharding import Mesh
from jax.sharding import PartitionSpec as P

BLOCK = 16
COL = ("col_0", "col_1")
ROW = ("row_0", "row_1", "row_2")
ROW_COL = ("row_0", "row_1", "row_2", "col_0", "col_1")


def sent_together(arrays, axis, dim, along):
    both = jnp.concatenate(arrays, axis=along)
    whole, at, finished = (lax.all_gather(both, axis, axis=dim, tiled=True), 0, [])
    for a in arrays:
        finished.append(lax.slice_in_dim(whole, at, at + a.shape[along], axis=along))
        at += a.shape[along]
    return tuple(finished)


def split_up(array, dim, size):
    lengths = array.shape
    pieces = array.reshape(*lengths[:dim], size, lengths[dim] // size, *lengths[dim + 1 :])
    return jnp.moveaxis(pieces, dim, 0)


def sum_at_owner(array, axis, dim):
    size = lax.axis_size(axis)
    pieces = lax.all_to_all(split_up(array, dim, size), axis, 0, 0, tiled=True)
    return jnp.sum(pieces.astype(jnp.float32), axis=0)


def by_axis(array, axes):
    return functools.reduce(lax.pmax, axes, array)


def fp4_values(packed):
    low_bits = jnp.bitwise_and(packed, 15)
    high_bits = jnp.bitwise_and(jnp.right_shift(packed, 4), 15)
    codes = jnp.stack([low_bits, high_bits], axis=-1).reshape(packed.shape[0], 2 * packed.shape[1])
    magnitude = jnp.bitwise_and(codes, 7).astype(jnp.float32)
    negative = jnp.right_shift(codes, 3).astype(jnp.float32)
    level = jnp.where(
        magnitude < 4.0,
        0.5 * magnitude,
        jnp.where(magnitude < 6.0, magnitude - 2.0, 2.0 * magnitude - 8.0),
    )
    return level * (1.0 - 2.0 * negative)


def e4m3_values(scale_codes):
    exponent = jnp.right_shift(scale_codes, 3)
    mantissa = jnp.bitwise_and(scale_codes, 7)
    power = jnp.left_shift(jnp.ones_like(exponent), exponent)
    normal_part = ((8 + mantissa) * power).astype(jnp.float32) / 1024.0
    subnormal = mantissa.astype(jnp.float32) / 512.0
    return jnp.where(exponent > 0, normal_part, subnormal)


def dequantize(packed, scale_codes):
    level = fp4_values(packed)
    row_total = level.shape[0]
    col_total = level.shape[1]
    block_scale = e4m3_values(scale_codes).T
    scaled = level.reshape(row_total, block_scale.shape[1], BLOCK) * block_scale[:, :, None]
    return scaled.reshape(row_total, col_total).astype(jnp.bfloat16)


def swiglu_grads(hidden_grad, gate_rows, up_rows):
    gate_value = gate_rows.astype(jnp.float32)
    up_value = up_rows.astype(jnp.float32)
    sigmoid_gate = jax.nn.sigmoid(gate_value)
    gate_grad = (
        hidden_grad * up_value * sigmoid_gate * (1.0 + gate_value * (1.0 - sigmoid_gate))
    ).astype(jnp.bfloat16)
    up_grad = (hidden_grad * gate_value * sigmoid_gate).astype(jnp.bfloat16)
    return (gate_grad, up_grad)


def per_device(
    out_grad,
    gate_act,
    up_act,
    gate_codes,
    gate_scales,
    up_codes,
    up_scales,
    down_codes,
    down_scales,
    tensor_scales,
):
    weight_down = dequantize(down_codes, down_scales)
    weight_gate = dequantize(gate_codes, gate_scales)
    weight_up = dequantize(up_codes, up_scales)
    grads_all = lax.all_gather(out_grad, COL, axis=0, tiled=True)
    hidden_grad = (
        lax.psum_scatter(
            jnp.dot(grads_all, weight_down, preferred_element_type=jnp.float32).astype(
                jnp.bfloat16
            ),
            ROW,
            scatter_dimension=0,
            tiled=True,
        ).astype(jnp.float32)
        * tensor_scales[2]
    )
    gate_part, up_part = swiglu_grads(hidden_grad, gate_act, up_act)
    gate_grad, up_grad = sent_together((gate_part, up_part), ROW, 0, 1)
    term = tensor_scales[0] * jnp.dot(gate_grad, weight_gate, preferred_element_type=jnp.float32)
    width_grad = sum_at_owner(
        (
            term
            + tensor_scales[1] * jnp.dot(up_grad, weight_up, preferred_element_type=jnp.float32)
        ).astype(jnp.bfloat16),
        COL,
        0,
    )
    largest = by_axis(jnp.max(jnp.abs(width_grad)), ROW_COL)
    grad_unit = (6.0 * width_grad / (largest + 1e-06)).astype(jnp.bfloat16)
    return (grad_unit, largest.reshape(1))


def solution(mesh):
    split = Mesh(mesh.devices.reshape(4, 2, 2, 2, 4), ("row_0", "row_1", "row_2", "col_0", "col_1"))
    placed = (
        P(COL, ROW),
        P(ROW, COL),
        P(ROW, COL),
        P(COL, ROW),
        P(ROW, COL),
        P(COL, ROW),
        P(ROW, COL),
        P(ROW, COL),
        P(COL, ROW),
        P(),
    )
    return jax.shard_map(
        per_device, mesh=split, in_specs=placed, out_specs=(P(COL, ROW), P()), check_vma=False
    )
```

profile of v0, /device:TPU:0, one launch (start us, length us, event | category | flops | bytes accessed | tf_op | source)
XLA Modules:
  0.0 392.9 jit_solution(14300256744165822752)
XLA Ops:
  7.2 0.0 all-gather.3.cloned.1.call-start
  7.2 0.7 all-gather.3.cloned.1.call-update
  7.9 0.0 reduce-scatter.4.cloned.1.call-start
  7.9 3.0 and_bitcast_fusion.5
  11.0 3.7 select_multiply_fusion.2
  14.7 15.4 %copy.28 = f32[512,1848,2]{0,2,1:T(2,128)} copy(f32[512,1848,2]{0,1,2:T(8,128)S(1)} %select_multiply_fusion.2) | data formatting | bytes 15138816 | tf_op jit(solution)/shard_map/mul | solution.py:51
  30.1 10.2 %reshape.105 = f32[512,3696]{0,1:T(8,128)} reshape(f32[512,1848,2]{0,2,1:T(2,128)} %copy.28) | data formatting | bytes 15138816 | tf_op jit(solution)/shard_map/mul | solution.py:51
  40.3 0.0 copy-done.3
  40.3 0.2 select_bitcast_fusion.2
  40.5 6.3 %fusion.7 = bf16[512,3696]{0,1:T(8,128)(2,1)} fusion(f32[512,3696]{0,1:T(8,128)} %reshape.105, f32[512,231]{0,1:T(8,128)S(1)} %select_bitcast_fusion.2), kind=kLoop, calls=%fused_computation.14 | loop fusion | flops 3784704 | bytes 11827200 | tf_op jit(solution)/shard_map/convert_element_type | solution.py:69
  46.8 5.2 %all-gather.3.cloned.1.call-done = bf16[1280,512]{1,0:T(8,128)(2,1)} async-done(((bf16[160,512]{1,0:T(8,128)(2,1)}), bf16[1280,512]{1,0:T(8,128)(2,1)}) %all-gather.3.cloned.1.call-update) | async-done | bytes 1310736 | tf_op jit(solution)/shard_map/all_gather | solution.py:98
  52.0 9.3 %fusion = bf16[1280,3696]{0,1:T(8,128)(2,1)} fusion(bf16[512,3696]{0,1:T(8,128)(2,1)} %fusion.7, bf16[1280,512]{1,0:T(8,128)(2,1)} %all-gather.3.cloned.1.call-done), kind=kOutput, calls=%fused_computation.1 | convolution fusion | flops 4849152000 | bytes 14557184 | tf_op jit(solution)/shard_map/dot_general | solution.py:101
  61.4 13.6 %copy.32 = bf16[1280,3696]{1,0:T(8,128)(2,1)} copy(bf16[1280,3696]{0,1:T(8,128)(2,1)} %fusion) | data formatting | bytes 18923520
  75.0 0.0 reduce-scatter.4.cloned.1.call-update
  75.0 0.0 all-gather.5.cloned.1.call-start
  75.0 0.6 copy-done.6
  75.6 0.6 fusion.28
  76.2 109.4 %reduce-scatter.4.cloned.1.call-done = bf16[80,3696]{1,0:T(8,128)(2,1)} async-done(((bf16[1280,3696]{1,0:T(8,128)(2,1)}), bf16[80,3696]{1,0:T(8,128)(2,1)}) %reduce-scatter.4.cloned.1.call-update) | async-done | bytes 591376 | tf_op jit(solution)/shard_map/reduce_scatter | solution.py:100
  185.7 2.3 fusion.25
  188.0 1.3 pad_maximum_fusion
  189.3 0.0 all-gather.5.cloned.1.call-update
  189.3 2.8 and_bitcast_fusion.3
  192.1 5.8 %select_multiply_fusion.1 = f32[3696,256,2]{1,0,2:T(8,128)} fusion(s32[3696,256,1]{1,0,2:T(8,128)S(1)} %get-tuple-element.7, s32[3696,256,1]{1,0,2:T(8,128)S(1)} %get-tuple-element.6), kind=kLoop, calls=%fused_computation.16 | loop fusion | flops 30277632 | bytes 15138816 | tf_op jit(solution)/shard_map/mul | solution.py:51
  197.9 12.6 %copy.30 = f32[3696,256,2]{0,2,1:T(2,128)} copy(f32[3696,256,2]{1,0,2:T(8,128)} %select_multiply_fusion.1) | data formatting | bytes 15138816 | tf_op jit(solution)/shard_map/mul | solution.py:51
  210.5 10.3 %reshape.106 = f32[3696,512]{0,1:T(8,128)} reshape(f32[3696,256,2]{0,2,1:T(2,128)} %copy.30) | data formatting | bytes 15138816 | tf_op jit(solution)/shard_map/mul | solution.py:51
  220.8 2.8 and_bitcast_fusion.1
  223.6 5.5 %select_multiply_fusion = f32[3696,256,2]{1,0,2:T(8,128)} fusion(s32[3696,256,1]{1,0,2:T(8,128)S(1)} %get-tuple-element.3, s32[3696,256,1]{1,0,2:T(8,128)S(1)} %get-tuple-element.2), kind=kLoop, calls=%fused_computation.15 | loop fusion | flops 30277632 | bytes 15138816 | tf_op jit(solution)/shard_map/mul | solution.py:51
  229.2 12.7 %copy.31 = f32[3696,256,2]{0,2,1:T(2,128)} copy(f32[3696,256,2]{1,0,2:T(8,128)} %select_multiply_fusion) | data formatting | bytes 15138816 | tf_op jit(solution)/shard_map/mul | solution.py:51
  241.8 10.3 %reshape.107 = f32[3696,512]{0,1:T(8,128)} reshape(f32[3696,256,2]{0,2,1:T(2,128)} %copy.31) | data formatting | bytes 15138816 | tf_op jit(solution)/shard_map/mul | solution.py:51
  252.1 0.2 select_bitcast_fusion.1
  252.3 0.0 slice-start.1
  252.3 6.0 %fusion.6 = bf16[3696,512]{0,1:T(8,128)(2,1)} fusion(f32[3696,512]{0,1:T(8,128)} %reshape.106, f32[3696,32]{0,1:T(8,128)S(1)} %select_bitcast_fusion.1), kind=kLoop, calls=%fused_computation.9 | loop fusion | flops 3784704 | bytes 11827200 | tf_op jit(solution)/shard_map/convert_element_type | solution.py:69
  258.3 0.2 select_bitcast_fusion
  258.4 0.0 slice-done
  258.4 0.0 slice-done.1
  258.5 2.5 fusion.5
  261.0 47.2 %all-gather.5.cloned.1.call-done = bf16[1280,7392]{1,0:T(8,128)(2,1)} async-done(((bf16[80,7392]{1,0:T(8,128)(2,1)}), bf16[1280,7392]{1,0:T(8,128)(2,1)}) %all-gather.5.cloned.1.call-update) | async-done | bytes 18923536 | tf_op jit(solution)/shard_map/all_gather | solution.py:17
  308.2 10.0 %fusion.8 = f32[1280,512]{1,0:T(8,128)S(1)} fusion(bf16[3696,512]{0,1:T(8,128)(2,1)} %fusion.6, bf16[1280,7392]{1,0:T(8,128)(2,1)} %all-gather.5.cloned.1.call-done, f32[]{:T(128)} %bitcast), kind=kOutput, calls=%fused_computation.30 | convolution fusion | flops 4845076480 | bytes 15925760 | tf_op jit(solution)/shard_map/dot_general | solution.py:112
  318.2 8.9 %fusion.17 = bf16[1280,512]{1,0:T(8,128)(2,1)S(1)} fusion(f32[1280,512]{1,0:T(8,128)S(1)} %fusion.8, bf16[3696,512]{0,1:T(8,128)(2,1)S(1)} %copy-done, bf16[1280,7392]{1,0:T(8,128)(2,1)} %all-gather.5.cloned.1.call-done, f32[]{:T(128)} %bitcast.11), kind=kOutput, calls=%fused_computation.33 | convolution fusion | flops 4846387200 | bytes 17220096 | tf_op jit(solution)/shard_map/dot_general | solution.py:116
  327.1 23.1 %all_to_all.5 = bf16[8,160,512]{2,1,0:T(8,128)(2,1)S(1)} all-to-all(bf16[8,160,512]{2,1,0:T(8,128)(2,1)S(1)} %bitcast.50), channel_id=1, replica_groups=mesh['row_0'=4,'row_1'=2,'row_2'=2,'col_0'=2,'col_1'=4] {'col_0','col_1'}, dimensions={0} | all-to-all | bytes 2621440 | tf_op jit(solution)/shard_map/all_to_all | solution.py:32
  350.2 0.2 convert_reduce_fusion
  350.4 0.6 abs_reduce_fusion
  351.0 9.2 %pmax.35 = f32[]{:T(128)} all-reduce(f32[]{:T(128)} %abs_reduce_fusion), channel_id=1, replica_groups=mesh['row_0'=4,'row_1'=2,'row_2'=2,'col_0'=2,'col_1'=4] {'row_0'}, use_global_device_ids=true, to_apply=%region_3.4 | all-reduce | flops 1 | bytes 8 | tf_op jit(solution)/shard_map/pmax | solution.py:37
  360.2 7.0 %pmax.36 = f32[]{:T(128)} all-reduce(f32[]{:T(128)} %pmax.35), channel_id=1, replica_groups=mesh['row_0'=4,'row_1'=2,'row_2'=2,'col_0'=2,'col_1'=4] {'row_1'}, use_global_device_ids=true, to_apply=%region_4.5 | all-reduce | flops 1 | bytes 8 | tf_op jit(solution)/shard_map/pmax | solution.py:37
  367.2 3.1 pmax.37
  370.3 5.5 %pmax.38 = f32[]{:T(128)} all-reduce(f32[]{:T(128)} %pmax.37), channel_id=1, replica_groups=mesh['row_0'=4,'row_1'=2,'row_2'=2,'col_0'=2,'col_1'=4] {'col_0'}, use_global_device_ids=true, to_apply=%region_6.7 | all-reduce | flops 1 | bytes 8 | tf_op jit(solution)/shard_map/pmax | solution.py:37
  375.9 9.2 %pmax.39 = f32[]{:T(128)} all-reduce(f32[]{:T(128)} %pmax.38), channel_id=1, replica_groups=mesh['row_0'=4,'row_1'=2,'row_2'=2,'col_0'=2,'col_1'=4] {'col_1'}, use_global_device_ids=true, to_apply=%region_7.8 | all-reduce | flops 1 | bytes 8 | tf_op jit(solution)/shard_map/pmax | solution.py:37
  385.7 0.7 divide_convert_fusion
  (14 shorter events, 0.0 us)
Async XLA Ops:
  7.2 44.9 %all-gather.3.cloned.1.call-start = ((), (), s32[]{:S(2)}) async-start(), calls=%async_computation.2 | async-start | bytes 1474560 | tf_op jit(solution)/shard_map/all_gather | solution.py:98
  7.9 177.8 %reduce-scatter.4.cloned.1.call-start = ((), (), s32[]{:S(2)}) async-start(), calls=%async_computation.4 | async-start | bytes 10096640 | tf_op jit(solution)/shard_map/reduce_scatter | solution.py:100
  30.1 10.2 %copy-start.3 = (s32[231,512]{1,0:T(8,128)S(1)}, s32[231,512]{1,0:T(8,128)}, u32[]{:S(2)}) copy-start(s32[231,512]{1,0:T(8,128)} %param.18) | copy-start | bytes 1419268
  75.0 0.7 copy-start.6
  75.0 110.7 %copy-start.1 = (bf16[80,3696]{1,0:T(8,128)(2,1)S(1)}, bf16[80,3696]{1,0:T(8,128)(2,1)}, u32[]{:S(2)}) copy-start(bf16[80,3696]{1,0:T(8,128)(2,1)} %param.11) | copy-start | bytes 1774084
  75.0 110.7 %copy-start.2 = (bf16[80,3696]{1,0:T(8,128)(2,1)S(1)}, bf16[80,3696]{1,0:T(8,128)(2,1)}, u32[]{:S(2)}) copy-start(bf16[80,3696]{1,0:T(8,128)(2,1)} %param.12) | copy-start | bytes 1774084
  75.0 233.2 %all-gather.5.cloned.1.call-start = ((), (), s32[]{:S(2)}) async-start(), calls=%async_computation.3 | async-start | bytes 20193280 | tf_op jit(solution)/shard_map/all_gather | solution.py:17
  241.8 10.3 %copy-start.4 = (s32[32,3696]{1,0:T(8,128)S(1)}, s32[32,3696]{1,0:T(8,128)}, u32[]{:S(2)}) copy-start(s32[32,3696]{1,0:T(8,128)} %param.14) | copy-start | bytes 1419268
  252.1 6.2 %copy-start.5 = (s32[32,3696]{1,0:T(8,128)S(1)}, s32[32,3696]{1,0:T(8,128)}, u32[]{:S(2)}) copy-start(s32[32,3696]{1,0:T(8,128)} %param.16) | copy-start | bytes 1419268
  252.1 6.3 %slice-start = ((s8[7602176]{0:T(1024)(128)(4,1)}), s8[4194304]{0:T(1024)(128)(4,1)S(1)}, s32[]{:S(2)}) async-start(s8[7602176]{0:T(1024)(128)(4,1)} %bitcast.48), calls=%async_computation.5 | async-start | bytes 8388608
  252.3 6.2 %slice-start.1 = ((s8[7602176]{0:T(1024)(128)(4,1)}), s8[3407872]{0:T(1024)(128)(4,1)S(1)}, s32[]{:S(2)}) async-start(s8[7602176]{0:T(1024)(128)(4,1)} %bitcast.48), calls=%async_computation.6 | async-start | bytes 6815744
  308.2 10.0 %copy-start = (bf16[3696,512]{0,1:T(8,128)(2,1)S(1)}, bf16[3696,512]{0,1:T(8,128)(2,1)}, u32[]{:S(2)}) copy-start(bf16[3696,512]{0,1:T(8,128)(2,1)} %fusion.5) | copy-start | bytes 11354116
Sparse Core Ops, SparseCore 0:
  9.6 42.3 all-gather.2
  75.1 110.5 reduce-scatter.3
  189.4 118.7 all-gather.4
where the time goes:
time: 395 us; the launch traced here: 393 us
  waiting for transfers between devices  163 us (41%)
  local copies, waits for them, and re-layouts  86.3 us (22%)
  blocking collectives  57.1 us (14%)
  other arithmetic  44.1 us (11%)
  matrix products  28.2 us (7%)
  between operations  14.5 us (4%)
    reduce_scatter x1, waiting for transfers between devices, per_device(): lax.psum_scatter(jnp.dot(grads_all, weight_down, preferred_element_type=j...  109 us
    mul x6, local copies, waits for them, and re-layouts, fp4_values(): return level * (1.0 - 2.0 * negative)  71.4 us
    all_gather x1, waiting for transfers between devices, sent_together(): lax.all_gather(both, axis, axis=dim, tiled=True)  47.2 us
    pmax x5, blocking collectives, by_axis(): return functools.reduce(lax.pmax, axes, array)  34 us
    all_to_all x1, blocking collectives, sum_at_owner(): pieces = lax.all_to_all(split_up(array, dim, size), axis, 0, 0, tiled=True)  23.1 us
    mul x3, other arithmetic, fp4_values(): return level * (1.0 - 2.0 * negative)  15.1 us
    convert_element_type x3, other arithmetic, dequantize(): return scaled.reshape(row_total, col_total).astype(jnp.bfloat16)  14.8 us
    unnamed x19, local copies, waits for them, and re-layouts  14.2 us
  transfers between devices with their start and end apart: 3, of which 3 were waited for; matrix products, arithmetic and copies ran while one was open for 28% of the time, Pallas kernels for 0%

commit v1 on v0

v1 whole, which is shorter than its diff:
```python
import functools

import jax
import jax.numpy as jnp
from jax import lax
from jax.experimental import pallas as pl
from jax.experimental.pallas import tpu as pltpu
from jax.sharding import Mesh
from jax.sharding import PartitionSpec as P


COL = ("yl", "z")
ROW = ("x", "yh", "core")
EVERY = ("x", "yh", "core", "yl", "z")
NEAR = 32
FAR = 80 - NEAR
BF16 = jnp.bfloat16
F32 = jnp.float32


def cost(flops, moved):
    return pl.CostEstimate(flops=int(flops), bytes_accessed=int(moved), transcendentals=0)


def params(mib=3):
    return pltpu.CompilerParams(vmem_limit_bytes=mib << 20)


SMEM = pl.BlockSpec(memory_space=pltpu.SMEM)
VMEM = pl.BlockSpec(memory_space=pltpu.VMEM)


def in_vmem(*arrays):
    return [pltpu.with_memory_space_constraint(a, pltpu.VMEM) for a in arrays]


def spans(n, step):
    return [slice(at, min(at + step, n)) for at in range(0, n, step)]


def each_span(n, step, body):
    def once(i, carry):
        body(pl.ds(pl.multiple_of(i * step, step), step))
        return carry

    lax.fori_loop(0, n // step, once, 0)
    if n % step:
        body(pl.ds(n // step * step, n % step))


def call(body, args, out_shape, scratch=(), smem=0, out_specs=None):
    return pl.pallas_call(
        body,
        in_specs=[SMEM] * smem + [VMEM] * (len(args) - smem),
        out_specs=out_specs or [VMEM] * len(out_shape),
        out_shape=[jax.ShapeDtypeStruct(*o) for o in out_shape],
        scratch_shapes=list(scratch),
        compiler_params=params(10),
        cost_estimate=cost(100000, 100000),
    )(*args)


def turn(a, k):
    return lax.ppermute(a, "x", [(i, (i + k) % 4) for i in range(4)])


def flip(a, axis):
    return lax.ppermute(a, axis, [(0, 1), (1, 0)])


def turn_z(a, k):
    return lax.ppermute(a, "z", [(i, (i + k) % 4) for i in range(4)])


def e4m3_values(codes):
    exponent = jnp.right_shift(codes, 3)
    mantissa = jnp.bitwise_and(codes, 7)
    power = jnp.left_shift(jnp.ones_like(exponent), exponent)
    normal = ((8 + mantissa) * power).astype(F32) * (1.0 / 1024.0)
    subnormal = mantissa.astype(F32) * (1.0 / 512.0)
    return jnp.where(exponent > 0, normal, subnormal)


def twice_levels(words, at):
    table = jnp.int32(0xC8643210 - (1 << 32))
    place = (words << 2 if at == 0 else words >> 2) & 28
    size = lax.shift_right_arithmetic(jnp.broadcast_to(table, words.shape), place) & 15
    return jnp.where((words & (8 << at)) != 0, -size, size).astype(F32)


def one_hot(shape, of_row, of_col):
    rows = lax.broadcasted_iota(jnp.int32, shape, 0)
    cols = lax.broadcasted_iota(jnp.int32, shape, 1)
    return jnp.where(of_row(rows) == of_col(cols), 1.0, 0.0).astype(BF16)


def spread(scales, words):
    mix = one_hot((scales.shape[0], words), lambda r: r, lambda c: c // 8)
    return lax.dot_general(scales, mix, (((0,), (0,)), ((), ())), preferred_element_type=F32)


def down_kernel(codes, scales, out, start):
    count, rows = out.shape[0] // 2, codes.shape[1]

    def mixer(n):
        return one_hot((2 * n, 2 * n), lambda r: (r >> 1) + n * (r & 1), lambda c: c)

    mix = mixer(128)

    def block(at, scale_at, out_at, n, mix):
        scale = e4m3_values(scales[pl.ds(start // 8 + scale_at, n // 8), :]) * 0.5
        scale = jnp.broadcast_to(scale[:, None, :], (n // 8, 8, rows)).reshape(n, rows)
        words = codes[pl.ds(start + at, n), :]
        low = (twice_levels(words, 0) * scale).astype(BF16)
        high = (twice_levels(words, 4) * scale).astype(BF16)
        if n % 16 == 0:
            both = jnp.dot(mix, jnp.concatenate([low, high]), preferred_element_type=F32)
        else:
            both = jnp.dot(mix[:, :n], low, preferred_element_type=F32)
            both += jnp.dot(mix[:, n:], high, preferred_element_type=F32)
        out[pl.ds(out_at, 2 * n), :] = both.astype(BF16)

    def once(i, carry):
        block(*(pl.multiple_of(i * k, k) for k in (128, 16, 256)), 128, mix)
        return carry

    lax.fori_loop(0, count // 128, once, 0)
    if count % 128:
        at = count // 128 * 128
        block(at, at // 8, 2 * at, count % 128, mixer(count % 128))


def dequantize_down(codes, scales, start, end):
    (out,) = call(
        functools.partial(down_kernel, start=start),
        in_vmem(codes, scales),
        [((2 * (end - start), codes.shape[1]), BF16)],
    )
    return out


def wide_kernel(codes, scales, out):
    count, words = codes.shape
    mix = one_hot((256, 256), lambda r: jnp.where(r < 128, 2 * r, 2 * r - 255), lambda c: c)

    def rows(w):
        scale = spread((e4m3_values(scales[:, w]) * 0.5).astype(BF16), words)
        for at in range(0, words, 128):
            cols = slice(at, at + 128)
            block = codes[w, cols]
            low = (twice_levels(block, 0) * scale[:, cols]).astype(BF16)
            high = (twice_levels(block, 4) * scale[:, cols]).astype(BF16)
            both = jnp.dot(jnp.concatenate([low, high], axis=1), mix, preferred_element_type=F32)
            out[w, 2 * at : 2 * at + 256] = both.astype(BF16)

    each_span(count, 512, rows)


def dequantize_wide(codes, scales):
    rows, words = codes.shape
    (out,) = call(wide_kernel, in_vmem(codes, scales), [((rows, 2 * words), BF16)])
    return out


def dot_rows(a, b):
    return lax.dot_general(a, b, (((1,), (1,)), ((), ())), preferred_element_type=F32)


def first_product(slot, grads, downs, near_side, far_blocks):
    k = downs[0].shape[1]
    n = downs[0].shape[0] + downs[2].shape[0]
    height = 4 * NEAR + FAR * len(far_blocks)

    def body(slot, g0, g1, g2, g3, own1, other1, own2, other2, *refs):
        near, *far, blocks, rows = refs
        for j, part in enumerate((g0, g1, g2, g3)):
            blocks[2 * j : 2 * j + 2] = part[...]
        for dx in range(4):
            rows[dx * NEAR : (dx + 1) * NEAR, :] = blocks[slot[2 * dx + near_side], :NEAR, :]
        for j, (dx, dy) in enumerate(far_blocks):
            at = 4 * NEAR + j * FAR
            rows[at : at + FAR, :] = blocks[slot[2 * dx + dy], NEAR:, :]

        def columns(own, other, w, to):
            total = dot_rows(rows[:, :k], own[w, :]) + dot_rows(rows[:, k:], other[w, :])
            total = total.astype(BF16)
            near[:, :, to] = total[: 4 * NEAR].reshape(4, NEAR, total.shape[1])
            for j, out in enumerate(far):
                at = 4 * NEAR + j * FAR
                out[:, to] = total[at : at + FAR]

        for w in spans(own1.shape[0], 1024):
            columns(own1, other1, w, w)
        base = own1.shape[0]
        for w in spans(own2.shape[0], 1024):
            columns(own2, other2, w, slice(base + w.start, base + w.stop))

    return call(
        body,
        [slot, *grads, *in_vmem(*downs)],
        [((4, NEAR, n), BF16)] + [((FAR, n), BF16)] * len(far_blocks),
        [pltpu.VMEM((8, 80, 2 * k), BF16), pltpu.VMEM((height, 2 * k), BF16)],
        smem=1,
    )


def add_kernel(*refs, groups):
    at = 0
    outs = refs[sum(groups) :]
    for out, count in zip(outs, groups):
        for w in spans(out.shape[1], 512):
            out[:, w] = sum(r[:, w].astype(F32) for r in refs[at : at + count]).astype(BF16)
        at += count


def add_up(groups):
    terms = [a for g in groups for a in g]
    rows, n = terms[0].shape
    return pl.pallas_call(
        functools.partial(add_kernel, groups=[len(g) for g in groups]),
        in_specs=[VMEM] * len(terms),
        out_specs=[VMEM] * len(groups),
        out_shape=[jax.ShapeDtypeStruct((rows, n), BF16)] * len(groups),
        compiler_params=params(10),
        cost_estimate=cost(rows * n * 1000, rows * n * 2 * (len(terms) + 1)),
    )(*terms)


def near_kernel(a, b, *outs):
    for k, out in enumerate(outs):
        for w in spans(out.shape[1], 512):
            out[:, w] = (a[k + 1, :, w].astype(F32) + b[k + 1, :, w].astype(F32)).astype(BF16)


def add_near(a, b):
    n = a.shape[2]
    return pl.pallas_call(
        near_kernel,
        in_specs=[VMEM] * 2,
        out_specs=[VMEM] * 3,
        out_shape=[jax.ShapeDtypeStruct((NEAR, n), BF16)] * 3,
        compiler_params=params(10),
        cost_estimate=cost(4 * NEAR * n * 1000, 4 * NEAR * n * 6),
        name="add_near",
    )(a, b)


def pair_of_grads(hidden, gate, up):
    gate = gate.astype(F32)
    up = up.astype(F32)
    sigma = jax.nn.sigmoid(gate)
    return (
        (hidden * up * sigma * (1.0 + gate * (1.0 - sigma))).astype(BF16),
        (hidden * gate * sigma).astype(BF16),
    )


def gates_kernel(scale, g, u, p1, y1, d1, d2, d3, o0, r1, r2, r3, near_h, far_h, out1, out2):
    near = (p1.at[0], y1.at[0], d1, d2, d3)
    far = (o0, r1, r2, r3)

    def columns(w):
        for terms, at, kept, out in ((near, 0, near_h, out1), (far, NEAR, far_h, out2)):
            h = out.shape[1]
            hidden = sum(r[:, w].astype(F32) for r in terms) * scale[2]
            kept[:, w] = hidden.astype(BF16)
            out[0, :, w], out[1, :, w] = pair_of_grads(hidden, g[at : at + h, w], u[at : at + h, w])

    each_span(g.shape[1], 256, columns)


def gates(scale, g, u, firsts, near, far):
    n = g.shape[1]
    return pl.pallas_call(
        gates_kernel,
        in_specs=[SMEM] + [VMEM] * 11,
        out_specs=[VMEM] * 4,
        out_shape=[
            jax.ShapeDtypeStruct((NEAR, n), BF16),
            jax.ShapeDtypeStruct((FAR, n), BF16),
            jax.ShapeDtypeStruct((2, NEAR, n), BF16),
            jax.ShapeDtypeStruct((2, FAR, n), BF16),
        ],
        compiler_params=params(10),
        cost_estimate=cost(80 * n * 5000, 80 * n * 2 * 9),
        name="gates",
    )(scale, g, u, *firsts, *near, *far)


def again(items, apart=()):
    count = len(items)
    n = items[0][0].shape[1]

    def body(*refs):
        outs = refs[2 * count : 3 * count]
        copies = refs[3 * count :]

        def columns(w):
            for j, out in enumerate(outs):
                hidden, acts = refs[2 * j : 2 * j + 2]
                h = hidden.shape[0]
                at = 0 if h == NEAR else NEAR
                both = pair_of_grads(
                    hidden[:, w].astype(F32), acts[0, at : at + h, w], acts[1, at : at + h, w]
                )
                out[0, :, w], out[1, :, w] = both
                for (item, which), copy in zip(apart, copies):
                    if item == j:
                        copy[:, w] = both[which]

        each_span(n, 256, columns)

    shapes = [((2, *i[0].shape), BF16) for i in items]
    shapes += [(items[item][0].shape, BF16) for item, _ in apart]
    return call(body, [a for item in items for a in item], shapes)


EARLY_NEAR = ((0, 0), (1, 0), (3, 0), (0, 1))
EARLY_FAR = ((0, 0), (0, 1))
LATE_NEAR = ((2, 0), (1, 1), (3, 1), (2, 1))
MIDDLE_FAR = ((1, 0), (1, 1), (3, 0), (3, 1))
LAST_FAR = ((2, 0), (2, 1))


def join(left, rows_g, rows_u):
    r = 0
    left = list(left)
    while left:
        a = left.pop(0)
        gate, up = (a, left.pop(0)) if len(a.shape) == 2 else (a.at[0], a.at[1])
        h = gate.shape[0]
        rows_g[r : r + h, :] = gate[...]
        rows_u[r : r + h, :] = up[...]
        r += h


def scaled(scale, rows_g, rows_u, gate_w, up_w, cols):
    n = gate_w.shape[0]
    cut = n // 256 * 256

    def product(rows, w):
        total = jnp.dot(rows[:, :cut], w[:cut, cols], preferred_element_type=F32)
        return total + jnp.dot(rows[:, cut:], w[cut:, cols], preferred_element_type=F32)

    return (scale[0] * product(rows_g, gate_w) + scale[1] * product(rows_u, up_w)).astype(BF16)


def second_kernel(scale, *refs):
    *left, own_g, own_u, other_g, other_u, out, rows_g, rows_u = refs
    join(left, rows_g, rows_u)
    width = own_g.shape[1]
    for base, gate_w, up_w in ((0, own_g, own_u), (width, other_g, other_u)):
        for at in range(0, width, 256):
            out[:, base + at : base + at + 256] = scaled(
                scale, rows_g, rows_u, gate_w, up_w, slice(at, at + 256)
            )


def second_product(scale, lefts, weights):
    n, width = weights[0].shape
    rows = sum(a.shape[1] for a in lefts)
    return pl.pallas_call(
        second_kernel,
        in_specs=[SMEM] + [VMEM] * (len(lefts) + 4),
        out_specs=VMEM,
        out_shape=jax.ShapeDtypeStruct((rows, 2 * width), BF16),
        scratch_shapes=[pltpu.VMEM((rows, n), BF16)] * 2,
        compiler_params=params(10),
        cost_estimate=cost(8 * rows * n * width, 8 * n * width + 4 * rows * n),
    )(scale, *lefts, *weights)


def near_last_kernel(scale, place, *refs):
    *left, own_g, own_u, other_g, other_u, early, z0, z1, z2, z3, rows_g, rows_u, blocks = refs
    join(left, rows_g, rows_u)
    width = own_g.shape[1]
    for j, (dx, dy) in enumerate(EARLY_NEAR):
        blocks[2 * dx + dy] = early[j * NEAR : (j + 1) * NEAR]
    for base, gate_w, up_w in ((0, own_g, own_u), (width, other_g, other_u)):
        total = scaled(scale, rows_g, rows_u, gate_w, up_w, slice(0, width))
        for j, (dx, dy) in enumerate(LATE_NEAR):
            blocks[2 * dx + dy, :, base : base + width] = total[j * NEAR : (j + 1) * NEAR]
    for k, out in enumerate((z0, z1, z2, z3)):
        for d in range(2):
            out[d] = blocks[place[16 + 2 * k + d]]


def near_last(scale, place, lefts, weights, early):
    n, width = weights[0].shape
    rows = 4 * NEAR
    return pl.pallas_call(
        near_last_kernel,
        in_specs=[SMEM] * 2 + [VMEM] * (len(lefts) + 5),
        out_specs=[VMEM] * 4,
        out_shape=[jax.ShapeDtypeStruct((2, NEAR, 2 * width), BF16)] * 4,
        scratch_shapes=[pltpu.VMEM((rows, n), BF16)] * 2
        + [pltpu.VMEM((8, NEAR, 2 * width), BF16)],
        compiler_params=params(10),
        cost_estimate=cost(8 * rows * n * width, 8 * n * width + 4 * rows * n),
        name="near_last",
    )(scale, place, *lefts, *weights, early)


def near_sum_kernel(z0, z1, z2, z3, keep, send):
    total = sum(z[...].astype(F32) for z in (z0, z1, z2, z3))
    keep[...] = total[0]
    send[...] = total[1].astype(BF16)


def near_sum(parts):
    shape = parts[0].shape[1:]
    return pl.pallas_call(
        near_sum_kernel,
        in_specs=[VMEM] * 4,
        out_specs=[VMEM] * 2,
        out_shape=[jax.ShapeDtypeStruct(shape, F32), jax.ShapeDtypeStruct(shape, BF16)],
        compiler_params=params(10),
        cost_estimate=cost(10000, 10000),
        name="near_sum",
    )(*parts)


def last_kernel(scale, place, *refs):
    *left, own_g, own_u, other_g, other_u, early, middle, out, rows_g, rows_u = refs
    join(left, rows_g, rows_u)
    width = own_g.shape[1]

    def put(rows, at, blocks, cols):
        for dx, dy in blocks:
            out[place[8 + 2 * dx + dy], :, cols] = rows[at : at + FAR]
            at += FAR

    both = slice(0, 2 * width)
    put(early[...], len(EARLY_NEAR) * NEAR, EARLY_FAR, both)
    put(middle[...], 0, MIDDLE_FAR, both)
    for base, gate_w, up_w in ((0, own_g, own_u), (width, other_g, other_u)):
        total = scaled(scale, rows_g, rows_u, gate_w, up_w, slice(0, width))
        put(total, 0, LAST_FAR, slice(base, base + width))


def last_product(scale, place, lefts, weights, done):
    n, width = weights[0].shape
    rows = sum(a.shape[1] for a in lefts)
    return pl.pallas_call(
        last_kernel,
        in_specs=[SMEM] * 2 + [VMEM] * (len(lefts) + 6),
        out_specs=VMEM,
        out_shape=jax.ShapeDtypeStruct((8, FAR, 2 * width), BF16),
        scratch_shapes=[pltpu.VMEM((rows, n), BF16)] * 2,
        compiler_params=params(10),
        cost_estimate=cost(8 * rows * n * width, 8 * n * width + 4 * rows * n),
        name="last",
    )(scale, place, *lefts, *weights, *done)


def whole(
    out_grad,
    gate_act,
    up_act,
    gate_codes,
    gate_scales,
    up_codes,
    up_scales,
    down_codes,
    down_scales,
    tensor_scales,
):
    x, yh, core, yl, z = (lax.axis_index(a) for a in EVERY)
    half = 80

    blocks, slots = [], []
    for dx in range(4):
        for dy in range(2):
            c = 2 * ((x + dx) % 4) + (yh ^ dy)
            blocks.append(c)
            slots.append(2 * ((z - c % 4) % 4) + ((c // 4) ^ yl))
    owners = []
    for dz in range(4):
        for dyl in range(2):
            c = 4 * (yl ^ dyl) + (z + dz) % 4
            owners.append(2 * ((c // 2 - x) % 4) + ((c % 2) ^ yh))
    place = jnp.stack(slots + blocks + owners + [core]).astype(jnp.int32)
    out_grad, place = lax.optimization_barrier((out_grad, place))

    def halves(place, grad, mine, theirs):
        at = pl.multiple_of(place[24] * half, 16)
        mine[...] = grad[pl.ds(at, half), :]
        theirs[...] = grad[pl.ds(half - at, half), :]

    def beside(a, b, out):
        out[:, : a.shape[1]] = a[...]
        out[:, a.shape[1] :] = b[...]

    def stacked(a, b, out):
        out[0] = a[...]
        out[1] = b[...]

    rows = (half, out_grad.shape[1])
    mine, theirs = call(halves, [place, out_grad], [(rows, BF16)] * 2, smem=1)
    theirs = flip(theirs, "core")
    (acts,) = call(stacked, [gate_act, up_act], [((2, *gate_act.shape), BF16)])
    (block,) = call(beside, [mine, theirs], [((half, 2 * rows[1]), BF16)])
    block_y = flip(block, "yl")
    acts3, acts1 = turn(acts, 1), turn(acts, 3)
    acts_y = flip(acts, "yh")
    (pair,) = call(stacked, [block, block_y], [((2, half, 2 * rows[1]), BF16)])
    grads = [pair] + [turn_z(pair, k) for k in (1, 2, 3)]

    words = down_codes.shape[1]
    cut = words * 5 // 9 // 128 * 128
    downs = []
    for span in ((0, cut), (cut, words)):
        down = dequantize_down(down_codes.T, down_scales, *span)
        downs += [down, flip(down, "core")]
    gate_own = dequantize_wide(gate_codes, gate_scales)
    gate_other = flip(gate_own, "core")
    up_own = dequantize_wide(up_codes, up_scales)
    up_other = flip(up_own, "core")

    y1, a2, b2 = first_product(place, grads, downs, 1, ((2, 0), (2, 1)))
    p1, b1, a3, a1, b3, o0, o1 = first_product(
        place, grads, downs, 0, ((1, 1), (3, 0), (1, 0), (3, 1), (0, 0), (0, 1))
    )

    got_a2 = turn(a2, 1)
    got_b2 = turn(b2, 3)
    got_y1 = flip(y1, "yh")
    got_b1 = turn(b1, 1)
    got_a3 = turn(a3, 3)
    s1, s3 = add_up(((a1, got_a2), (b3, got_b2)))
    got_a1 = turn(s1, 1)
    got_b3 = turn(s3, 3)
    d = add_near(p1, got_y1)
    got_d = [turn(d[k - 1], k) for k in (1, 2, 3)]
    (t1,) = add_up(((o1, got_b1, got_b3),))
    got_t = flip(t1, "yh")
    near_h, far_h, near, far = gates(
        tensor_scales, gate_act, up_act, (p1, got_y1), got_d, (o0, got_a3, got_a1, got_t)
    )

    far_y = flip(far_h, "yh")
    n3, n1 = turn(near_h, 1), turn(near_h, 3)
    m0 = flip(near_h, "yh")
    f3, f1 = turn(far_h, 1), turn(far_h, 3)
    n3, n1, n3_gate, n1_up = again(((n3, acts3), (n1, acts1)), ((0, 0), (1, 1)))
    n2 = turn(n3_gate, 1), turn(n1_up, 3)
    (far_y,) = again(((far_y, acts_y),))
    f3, f1, m0 = again(((f3, acts3), (f1, acts1), (m0, acts_y)))
    m1, m3 = flip(n1, "yh"), flip(n3, "yh")
    m2 = flip(n2[0], "yh"), flip(n2[1], "yh")
    h3, h1 = turn(far_y, 1), turn(far_y, 3)
    f2, h2 = turn(f3, 1), turn(h1, 3)

    weights = (gate_own, up_own, gate_other, up_other)
    early = second_product(tensor_scales, (near, n1, n3, m0, far, far_y), weights)
    middle = second_product(tensor_scales, (f1, h1, f3, h3), weights)

    parts = near_last(tensor_scales, place, (*n2, m1, m3, *m2), weights, early)
    parts = [parts[0]] + [turn_z(parts[k], k) for k in (1, 2, 3)]
    near_keep, near_send = near_sum(parts)
    near_got = flip(near_send, "yl")
    far_parts = last_product(tensor_scales, place, (f2, h2), weights, (early, middle))
    far_got = lax.all_to_all(far_parts, COL, 0, 0, tiled=True)
    width = far_got.shape[2] // 2

    def totals(far, keep, near, kept, other, largest):
        near_total = keep[...] + near[...].astype(F32)
        far_total = sum(far[j].astype(F32) for j in range(8))
        for out, cols in ((kept, slice(0, width)), (other, slice(width, 2 * width))):
            out[:NEAR] = near_total[:, cols]
            out[NEAR:] = far_total[:, cols]
        top = jnp.maximum(jnp.max(jnp.abs(near_total)), jnp.max(jnp.abs(far_total)))
        largest[...] = jnp.full(largest.shape, top, F32)

    kept, other, largest = call(
        totals, [far_got, near_keep, near_got], [((half, width), F32)] * 2 + [((128, 1, 128), F32)]
    )
    got = flip(other, "core")
    largest = lax.all_to_all(largest, EVERY, 0, 0, tiled=True)

    def scale_up(place, largest, kept, got, grad_unit, grad_amax):
        top = jnp.max(largest[...])
        at = pl.multiple_of(place[24] * half, 16)
        grad_unit[pl.ds(at, half), :] = (6.0 * kept[...] / (top + 1e-06)).astype(BF16)
        grad_unit[pl.ds(half - at, half), :] = (6.0 * got[...] / (top + 1e-06)).astype(BF16)
        grad_amax[0] = top

    return call(
        scale_up,
        [place, largest, kept, got],
        [((2 * half, width), BF16), ((1,), F32)],
        smem=1,
        out_specs=[VMEM, SMEM],
    )


def solution(mesh):
    split = Mesh(mesh.devices.reshape(4, 2, 2, 2, 4), EVERY)
    placed = (
        P(COL, ROW),
        P(ROW, COL),
        P(ROW, COL),
        P(COL, ROW),
        P(ROW, COL),
        P(COL, ROW),
        P(ROW, COL),
        P(ROW, COL),
        P(COL, ROW),
        P(),
    )
    return jax.shard_map(
        whole, mesh=split, in_specs=placed, out_specs=(P(COL, ROW), P()), check_vma=False
    )
```

time: 395 us -> 283 us (0.72)
  local copies, waits for them, and re-layouts: 86.3 us -> 11.5 us
  starting transfers between devices: 0.12 us -> 59.1 us
  Pallas kernels: 0 us -> 51.1 us
  other arithmetic: 44.1 us -> 0 us
  blocking collectives: 57.1 us -> 17.1 us
  matrix products: 28.2 us -> 0 us
  waiting for transfers between devices: 163 us -> 142 us
  between operations: 14.5 us -> 1.18 us
    ppermute x0 -> x44, waiting for transfers between devices: none -> 142 us  [the longest x21 89.8 us: turn(): return lax.ppermute(a, 'x', [(i, (i + k) % 4) for i in range(4)])]
    reduce_scatter x1 -> x0, waiting for transfers between devices: 109 us -> none  [per_device(): lax.psum_scatter(jnp.dot(grads_all, weight_down, preferred_element_type=j...]
    mul x6 -> x0, local copies, waits for them, and re-layouts: 71.4 us -> none  [fp4_values(): return level * (1.0 - 2.0 * negative)]
    ppermute x0 -> x44, starting transfers between devices: none -> 55.5 us  [the longest x21 23.7 us: turn(): return lax.ppermute(a, 'x', [(i, (i + k) % 4) for i in range(4)])]
    all_gather x2 -> x0, waiting for transfers between devices: 52.4 us -> none  [the longest x1 47.2 us: sent_together(): lax.all_gather(both, axis, axis=dim, tiled=True)]
    pallas_call x0 -> x24, Pallas kernels: none -> 51.1 us  [the longest x15 33.4 us: call(): pl.pallas_call(body, in_specs=[SMEM] * smem + [VMEM] * (len(args) - smem)...]
    pmax x5 -> x0, blocking collectives: 34 us -> none  [by_axis(): return functools.reduce(lax.pmax, axes, array)]
    dot_general x3 -> x0, matrix products: 28.2 us -> none  [the longest x1 9.98 us: per_device(): jnp.dot(gate_grad, weight_gate, preferred_element_type=jnp.float32)]
  transfers between devices with their start and end apart: 3 -> 45, of which waited for: 3 -> 25; matrix products, arithmetic and copies ran while one was open for 28% -> 0% of each run, Pallas kernels for 0% -> 15%
where the time goes in v1:
time: 283 us; the launch traced here: 282 us
  waiting for transfers between devices  142 us (50%)
  starting transfers between devices  59.1 us (21%)
  Pallas kernels  51.1 us (18%)
  blocking collectives  17.1 us (6%)
  local copies, waits for them, and re-layouts  11.5 us (4%)
    ppermute x21, waiting for transfers between devices, turn(): return lax.ppermute(a, 'x', [(i, (i + k) % 4) for i in range(4)])  89.8 us
    ppermute x17, waiting for transfers between devices, flip(): return lax.ppermute(a, axis, [(0, 1), (1, 0)])  35.1 us
    pallas_call x15, Pallas kernels, call(): pl.pallas_call(body, in_specs=[SMEM] * smem + [VMEM] * (len(args) - smem)...  33.4 us
    ppermute x21, starting transfers between devices, turn(): return lax.ppermute(a, 'x', [(i, (i + k) % 4) for i in range(4)])  23.7 us
    ppermute x17, starting transfers between devices, flip(): return lax.ppermute(a, axis, [(0, 1), (1, 0)])  18.9 us
    all_to_all x1, blocking collectives, whole(): largest = lax.all_to_all(largest, EVERY, 0, 0, tiled=True)  17.1 us
    ppermute x6, waiting for transfers between devices, turn_z(): return lax.ppermute(a, 'z', [(i, (i + k) % 4) for i in range(4)])  16.7 us
    ppermute x6, starting transfers between devices, turn_z(): return lax.ppermute(a, 'z', [(i, (i + k) % 4) for i in range(4)])  12.9 us
  transfers between devices with their start and end apart: 45, of which 25 were waited for; matrix products, arithmetic and copies ran while one was open for 0% of the time, Pallas kernels for 15%

profile of v1, /device:TPU:0, one launch (start us, length us, event | category | flops | bytes accessed | tf_op | source)
XLA Modules:
  0.0 281.7 jit_solution(8927479428546069162)
XLA Ops:
  3.7 3.4 %shard_map.116.own1 = bf16[2048,512]{1,0:T(8,128)(2,1)S(1)} custom-call(s32[1848,512]{1,0:T(8,128)S(1)} %bitcast.26, s32[231,512]{1,0:T(8,128)S(1)} %copy-done.11), custom_call_target="tpu_custom_call" | custom-call | flops 100000 | bytes 100000 | tf_op jit(solution)/shard_map/pallas_call | solution.py:52
  7.2 4.0 %shard_map.117.own2 = bf16[1648,512]{1,0:T(8,128)(2,1)} custom-call(s32[1848,512]{1,0:T(8,128)S(1)} %bitcast.27, s32[231,512]{1,0:T(8,128)S(1)} %copy-done.11), custom_call_target="tpu_custom_call" | custom-call | flops 100000 | bytes 100000 | tf_op jit(solution)/shard_map/pallas_call | solution.py:52
  12.5 2.8 collective-permute-done.b
  17.0 4.8 %collective-permute-done.1.b = bf16[80,1024]{1,0:T(8,128)(2,1)S(1)} collective-permute-done((bf16[80,1024]{1,0:T(8,128)(2,1)S(1)}, bf16[80,1024]{1,0:T(8,128)(2,1)S(1)}, u32[]{:S(2)}, u32[]{:S(2)}) %collective-permute-start.1) | collective-permute-done | bytes 163872 | tf_op jit(solution)/shard_map/ppermute | solution.py:68
  21.8 2.1 collective-permute-start.2
  23.9 3.6 %collective-permute-start.3 = (bf16[2,80,1024]{2,1,0:T(8,128)(2,1)S(1)}, bf16[2,80,1024]{2,1,0:T(8,128)(2,1)S(1)}, u32[]{:S(2)}, u32[]{:S(2)}) collective-permute-start(bf16[2,80,1024]{2,1,0:T(8,128)(2,1)S(1)} %shard_map.115.g0), channel_id=1, source_target_pairs={{0,2},{1,3},{2,0},{3,1},{4,6},{5,7},{6,4},{7,5},{8,10},{9,11},{10,... | collective-permute-start | bytes 983048 | tf_op jit(solution)/shard_map/ppermute | solution.py:72
  28.5 5.2 %collective-permute-done.2.g1 = bf16[2,80,1024]{2,1,0:T(8,128)(2,1)S(1)} collective-permute-done((bf16[2,80,1024]{2,1,0:T(8,128)(2,1)S(1)}, bf16[2,80,1024]{2,1,0:T(8,128)(2,1)S(1)}, u32[]{:S(2)}, u32[]{:S(2)}) %collective-permute-start.2) | collective-permute-done | bytes 327712 | tf_op jit(solution)/shard_map/ppermute | solution.py:72
  33.7 7.9 %collective-permute-done.3.g2 = bf16[2,80,1024]{2,1,0:T(8,128)(2,1)S(1)} collective-permute-done((bf16[2,80,1024]{2,1,0:T(8,128)(2,1)S(1)}, bf16[2,80,1024]{2,1,0:T(8,128)(2,1)S(1)}, u32[]{:S(2)}, u32[]{:S(2)}) %collective-permute-start.3) | collective-permute-done | bytes 327712 | tf_op jit(solution)/shard_map/ppermute | solution.py:72
  41.7 5.2 %shard_map.119 = (bf16[4,32,3696]{2,1,0:T(8,128)(2,1)S(1)}, bf16[48,3696]{1,0:T(8,128)(2,1)S(1)}, bf16[48,3696]{1,0:T(8,128)(2,1)S(1)}) custom-call(s32[25]{0:T(128)S(1)} %stack.103.place.slot, bf16[2,80,1024]{2,1,0:T(8,128)(2,1)S(1)} %shard_map.115.g0, bf16[2,80,1024]{2,1,0:T(8,128)(2,1)S(1)} %collective-permute-done.2.g1, ...), custom_call_target="tpu_custom_call" | custom-call | flops 100000 | bytes 100000 | tf_op jit(solution)/shard_map/pallas_call | solution.py:52
  46.9 3.3 %collective-permute-start.7 = (bf16[4,32,3696]{2,1,0:T(8,128)(2,1)S(1)}, bf16[4,32,3696]{2,1,0:T(8,128)(2,1)S(1)}, u32[]{:S(2)}, u32[]{:S(2)}) collective-permute-start(bf16[4,32,3696]{2,1,0:T(8,128)(2,1)S(1)} %get-tuple-element.46), channel_id=1, source_target_pairs={{0,16},{16,0},{1,17},{17,1},{2,18},{18,2},{3,19},{19,3},{4,20},{20... | collective-permute-start | bytes 2838536 | tf_op jit(solution)/shard_map/ppermute | solution.py:68
  50.2 4.8 %shard_map.125.refs_6_.refs_4_.refs_2_ = bf16[3696,512]{1,0:T(8,128)(2,1)S(1)} custom-call(s32[3696,256]{1,0:T(8,128)S(1)} %copy-done.9, s32[32,3696]{1,0:T(8,128)S(1)} %copy-done.14), custom_call_target="tpu_custom_call" | custom-call | flops 100000 | bytes 100000 | tf_op jit(solution)/shard_map/pallas_call | solution.py:52
  55.2 4.8 %shard_map.126.refs_7_.refs_5_.refs_3_ = bf16[3696,512]{1,0:T(8,128)(2,1)S(1)} custom-call(s32[3696,256]{1,0:T(8,128)S(1)} %copy-done.10, s32[32,3696]{1,0:T(8,128)S(1)} %copy-done.15), custom_call_target="tpu_custom_call" | custom-call | flops 100000 | bytes 100000 | tf_op jit(solution)/shard_map/pallas_call | solution.py:52
  63.8 6.2 %shard_map.118 = (bf16[4,32,3696]{2,1,0:T(8,128)(2,1)S(1)}, bf16[48,3696]{1,0:T(8,128)(2,1)S(1)}, bf16[48,3696]{1,0:T(8,128)(2,1)S(1)}, bf16[48,3696]{1,0:T(8,12...) custom-call(s32[25]{0:T(128)S(1)} %stack.103.place.slot, ...), custom_call_target="tpu_custom_call" | custom-call | flops 100000 | bytes 100000 | tf_op jit(solution)/shard_map/pallas_call | solution.py:52
  70.0 2.1 collective-permute-done.12.refs_1_
  72.6 3.0 %collective-permute-start.16 = (bf16[48,3696]{1,0:T(8,128)(2,1)S(1)}, bf16[48,3696]{1,0:T(8,128)(2,1)S(1)}, u32[]{:S(2)}, u32[]{:S(2)}) collective-permute-start(bf16[48,3696]{1,0:T(8,128)(2,1)S(1)} %get-tuple-element.59), channel_id=1, source_target_pairs={{0,96},{32,0},{64,32},{96,64},{1,97},{33,1},{65,33},{97,65},{2,98}... | collective-permute-start | bytes 1064456 | tf_op jit(solution)/shard_map/ppermute | solution.py:64
  75.6 7.2 %collective-permute-done.15.refs_1_ = bf16[48,3696]{1,0:T(8,128)(2,1)S(1)} collective-permute-done((bf16[48,3696]{1,0:T(8,128)(2,1)S(1)}, bf16[48,3696]{1,0:T(8,128)(2,1)S(1)}, u32[]{:S(2)}, u32[]{:S(2)}) %collective-permute-start.15) | collective-permute-done | bytes 354848 | tf_op jit(solution)/shard_map/ppermute | solution.py:64
  85.5 5.8 %collective-permute-done.11.r1 = bf16[48,3696]{1,0:T(8,128)(2,1)S(1)} collective-permute-done((bf16[48,3696]{1,0:T(8,128)(2,1)S(1)}, bf16[48,3696]{1,0:T(8,128)(2,1)S(1)}, u32[]{:S(2)}, u32[]{:S(2)}) %collective-permute-start.11) | collective-permute-done | bytes 354848 | tf_op jit(solution)/shard_map/ppermute | solution.py:64
  91.4 2.2 collective-permute-start.10
  94.8 2.6 collective-permute-done.10.d3
  99.2 31.9 %collective-permute-done.8.d1 = bf16[32,3696]{1,0:T(8,128)(2,1)S(1)} collective-permute-done((bf16[32,3696]{1,0:T(8,128)(2,1)S(1)}, bf16[32,3696]{1,0:T(8,128)(2,1)S(1)}, u32[]{:S(2)}, u32[]{:S(2)}) %collective-permute-start.8) | collective-permute-done | bytes 236576 | tf_op jit(solution)/shard_map/ppermute | solution.py:64
  133.0 3.2 %collective-permute-start.25 = (bf16[48,3696]{1,0:T(8,128)(2,1)S(1)}, bf16[48,3696]{1,0:T(8,128)(2,1)S(1)}, u32[]{:S(2)}, u32[]{:S(2)}) collective-permute-start(bf16[48,3696]{1,0:T(8,128)(2,1)S(1)} %get-tuple-element.60), channel_id=1, source_target_pairs={{0,16},{16,0},{1,17},{17,1},{2,18},{18,2},{3,19},{19,3},{4,20},{20... | collective-permute-start | bytes 1064456 | tf_op jit(solution)/shard_map/ppermute | solution.py:68
  136.3 16.6 %collective-permute-done.21.refs_3_ = bf16[2,80,3696]{2,1,0:T(8,128)(2,1)S(1)} collective-permute-done((bf16[2,80,3696]{2,1,0:T(8,128)(2,1)S(1)}, bf16[2,80,3696]{2,1,0:T(8,128)(2,1)S(1)}, u32[]{:S(2)}, u32[]{:S(2)}) %collective-permute-start.21) | collective-permute-done | bytes 1182752 | tf_op jit(solution)/shard_map/ppermute | solution.py:64
  153.2 8.4 %collective-permute-done.23.refs_5_.refs_1_ = bf16[2,80,3696]{2,1,0:T(8,128)(2,1)S(1)} collective-permute-done((bf16[2,80,3696]{2,1,0:T(8,128)(2,1)S(1)}, bf16[2,80,3696]{2,1,0:T(8,128)(2,1)S(1)}, u32[]{:S(2)}, u32[]{:S(2)}) %collective-permute-start.23) | collective-permute-done | bytes 1182752 | tf_op jit(solution)/shard_map/ppermute | solution.py:68
  162.5 3.5 %collective-permute-done.25.refs_0_ = bf16[48,3696]{1,0:T(8,128)(2,1)S(1)} collective-permute-done((bf16[48,3696]{1,0:T(8,128)(2,1)S(1)}, bf16[48,3696]{1,0:T(8,128)(2,1)S(1)}, u32[]{:S(2)}, u32[]{:S(2)}) %collective-permute-start.25) | collective-permute-done | bytes 354848 | tf_op jit(solution)/shard_map/ppermute | solution.py:68
  166.4 2.1 collective-permute-done.22.refs_4_
  169.6 2.6 collective-permute-done.18.refs_0_
  172.4 4.7 %collective-permute-done.20.refs_2_ = bf16[48,3696]{1,0:T(8,128)(2,1)S(1)} collective-permute-done((bf16[48,3696]{1,0:T(8,128)(2,1)S(1)}, bf16[48,3696]{1,0:T(8,128)(2,1)S(1)}, u32[]{:S(2)}, u32[]{:S(2)}) %collective-permute-start.20) | collective-permute-done | bytes 354848 | tf_op jit(solution)/shard_map/ppermute | solution.py:64
  179.3 2.6 collective-permute-done.30.refs_0_
  182.0 8.0 %collective-permute-done.31.refs_2_ = bf16[32,3696]{1,0:T(8,128)(2,1)S(1)} collective-permute-done((bf16[32,3696]{1,0:T(8,128)(2,1)S(1)}, bf16[32,3696]{1,0:T(8,128)(2,1)S(1)}, u32[]{:S(2)}, u32[]{:S(2)}) %collective-permute-start.31) | collective-permute-done | bytes 236576 | tf_op jit(solution)/shard_map/ppermute | solution.py:64
  190.0 4.1 %collective-permute-start.24 = (bf16[2,48,3696]{2,1,0:T(8,128)(2,1)S(1)}, bf16[2,48,3696]{2,1,0:T(8,128)(2,1)S(1)}, u32[]{:S(2)}, u32[]{:S(2)}) collective-permute-start(bf16[2,48,3696]{2,1,0:T(8,128)(2,1)S(1)} %get-tuple-element.62.refs_2_), channel_id=1, source_target_pairs={{0,32},{32,64},{64,96},{96,0},{1,33},{33,65},{65,97},{97,1},{2,34}... | collective-permute-start | bytes 2128904 | tf_op jit(solution)/shard_map/ppermute | solution.py:64
  197.1 3.1 %collective-permute-start.36 = (bf16[2,32,3696]{2,1,0:T(8,128)(2,1)S(1)}, bf16[2,32,3696]{2,1,0:T(8,128)(2,1)S(1)}, u32[]{:S(2)}, u32[]{:S(2)}) collective-permute-start(bf16[2,32,3696]{2,1,0:T(8,128)(2,1)S(1)} %get-tuple-element.65.refs_2_), channel_id=1, source_target_pairs={{0,16},{16,0},{1,17},{17,1},{2,18},{18,2},{3,19},{19,3},{4,20},{20... | collective-permute-start | bytes 1419272 | tf_op jit(solution)/shard_map/ppermute | solution.py:68
  200.3 4.4 %shard_map.128.refs_6_.refs_10_ = bf16[224,1024]{1,0:T(8,128)(2,1)S(1)} custom-call(f32[3]{0:T(128)S(1)} %copy-done.17, bf16[2,32,3696]{2,1,0:T(8,128)(2,1)S(1)} %get-tuple-element.63.refs_0_, bf16[2,32,3696]{2,1,0:T(8,128)(2,1)S(1)} %get-tuple-element.64.refs_1_, bf16[2,32,3696]{2,1,0:T(8,128)(2,1)S(1)} %get-tuple-element.65.refs_2_, ...), custom_call_target="tpu_custom_call" | custom-call | flops 3391094784 | bytes 18450432 | tf_op jit(solution)/shard_map/pallas_call | solution.py:362
  206.6 5.6 %collective-permute-done.24.refs_0_ = bf16[2,48,3696]{2,1,0:T(8,128)(2,1)S(1)} collective-permute-done((bf16[2,48,3696]{2,1,0:T(8,128)(2,1)S(1)}, bf16[2,48,3696]{2,1,0:T(8,128)(2,1)S(1)}, u32[]{:S(2)}, u32[]{:S(2)}) %collective-permute-start.24) | collective-permute-done | bytes 709664 | tf_op jit(solution)/shard_map/ppermute | solution.py:64
  212.2 4.1 %shard_map.129.refs_7_ = bf16[192,1024]{1,0:T(8,128)(2,1)S(1)} custom-call(f32[3]{0:T(128)S(1)} %copy-done.17, bf16[2,48,3696]{2,1,0:T(8,128)(2,1)S(1)} %get-tuple-element.68.refs_0_, bf16[2,48,3696]{2,1,0:T(8,128)(2,1)S(1)} %collective-permute-done.26.refs_1_, bf16[2,48,3696]{2,1,0:T(8,128)(2,1)S(1)} %get-tuple-element.62.refs_2_, ...), custom_call_target="tpu_custom_call" | custom-call | flops 2906652672 | bytes 17977344 | tf_op jit(solution)/shard_map/pallas_call | solution.py:362
  216.3 4.0 %last.1 = bf16[8,48,1024]{2,1,0:T(8,128)(2,1)} custom-call(f32[3]{0:T(128)S(1)} %copy-done.17, s32[25]{0:T(128)S(1)} %stack.103.place.slot, bf16[2,48,3696]{2,1,0:T(8,128)(2,1)S(1)} %collective-permute-done.24.refs_0_, bf16[2,48,3696]{2,1,0:T(8,128)(2,1)S(1)} %collective-permute-done.27.refs_1_, bf16[3696,512]{1,0:T(8,128)(2,1)S(1)} %shard_map.125.refs_6_.refs_4_.refs_2_, ...), custom_call_target="tpu_custom_call" | custom-call | flops 1453326336 | bytes 16558080 | tf_op jit(solution)/shard_map/last/pallas_call | solution.py:444
  220.4 3.6 %all-to-all-start = ((bf16[8,48,1024]{2,1,0:T(8,128)(2,1)}), bf16[8,48,1024]{2,1,0:T(8,128)(2,1)S(1)}, u32[]{:S(2)}, u32[]{:S(2)}) async-start(bf16[8,48,1024]{2,1,0:T(8,128)(2,1)} %last.1), calls=%async_computation | async-start | bytes 1572864 | tf_op jit(solution)/shard_map/all_to_all | solution.py:563
  227.6 6.8 %collective-permute-done.37.refs_4_ = bf16[32,3696]{1,0:T(8,128)(2,1)S(1)} collective-permute-done((bf16[32,3696]{1,0:T(8,128)(2,1)S(1)}, bf16[32,3696]{1,0:T(8,128)(2,1)S(1)}, u32[]{:S(2)}, u32[]{:S(2)}) %collective-permute-start.37) | collective-permute-done | bytes 236576 | tf_op jit(solution)/shard_map/ppermute | solution.py:68
  234.4 2.5 collective-permute-done.38.refs_5_
  237.0 2.1 copy-done.1
  239.0 2.1 copy-done.3
  241.1 2.1 copy-done.5
  243.2 2.1 copy-done.7
  245.2 3.2 %near_last.1 = (bf16[2,32,1024]{2,1,0:T(8,128)(2,1)S(1)}, bf16[2,32,1024]{2,1,0:T(8,128)(2,1)S(1)}, bf16[2,32,1024]{2,1,0:T(8,128)(2,1)S(1)}, bf16[2,32,1024]{2,1,0:T(8,128)(2,1)S(1)}) custom-call(f32[3]{0:T(128)S(1)} %copy-done.17, s32[25]{0:T(128)S(1)} %stack.103.place.slot, bf16[32,3696]{1,0:T(8,128)(2,1)S(1)} %collective-permute-done.33.refs_0_, ...), custom_call_target="tpu_custom_call" | custom-call | flops 1937768448 | bytes 17031168 | tf_op jit(solution)/shard_map/near_last/pallas_call | solution.py:391
  248.4 2.1 collective-permute-start.39
  250.5 2.8 collective-permute-start.40
  254.8 2.9 %collective-permute-done.40.z2 = bf16[2,32,1024]{2,1,0:T(8,128)(2,1)S(1)} collective-permute-done((bf16[2,32,1024]{2,1,0:T(8,128)(2,1)S(1)}, bf16[2,32,1024]{2,1,0:T(8,128)(2,1)S(1)}, u32[]{:S(2)}, u32[]{:S(2)}) %collective-permute-start.40) | collective-permute-done | bytes 131104 | tf_op jit(solution)/shard_map/ppermute | solution.py:72
  259.3 3.4 %collective-permute-done.42.near = bf16[32,1024]{1,0:T(8,128)(2,1)S(1)} collective-permute-done((bf16[32,1024]{1,0:T(8,128)(2,1)S(1)}, bf16[32,1024]{1,0:T(8,128)(2,1)S(1)}, u32[]{:S(2)}, u32[]{:S(2)}) %collective-permute-start.42) | collective-permute-done | bytes 65568 | tf_op jit(solution)/shard_map/ppermute | solution.py:68
  263.0 17.1 %all_to_all.10.largest = f32[128,1,128]{2,1,0:T(1,128)S(1)} all-to-all(f32[128,1,128]{2,1,0:T(1,128)S(1)} %get-tuple-element.77), channel_id=1, replica_groups=mesh['x'=4,'yh'=2,'core'=2,'yl'=2,'z'=4] {'x','yh','core','yl','z'}, dimensions={0} | all-to-all | bytes 131072 | tf_op jit(solution)/shard_map/all_to_all | solution.py:579
  (104 shorter events, 37.8 us)
Async XLA Ops:
  7.1 34.5 %collective-permute-start.5 = (bf16[2048,512]{1,0:T(8,128)(2,1)S(1)}, bf16[2048,512]{1,0:T(8,128)(2,1)}, u32[]{:S(2)}, u32[]{:S(2)}) collective-permute-start(bf16[2048,512]{1,0:T(8,128)(2,1)S(1)} %shard_map.116.own1), channel_id=1, source_target_pairs={{0,8},{8,0},{1,9},{9,1},{2,10},{10,2},{3,11},{11,3},{4,12},{12,4},... | collective-permute-start | bytes 6291464 | tf_op jit(solution)/shard_map/ppermute | solution.py:68
  11.2 30.5 %collective-permute-start.6 = (bf16[1648,512]{1,0:T(8,128)(2,1)}, bf16[1648,512]{1,0:T(8,128)(2,1)}, u32[]{:S(2)}, u32[]{:S(2)}) collective-permute-start(bf16[1648,512]{1,0:T(8,128)(2,1)} %shard_map.117.own2), channel_id=1, source_target_pairs={{0,8},{8,0},{1,9},{9,1},{2,10},{10,2},{3,11},{11,3},{4,12},{12,4},... | collective-permute-start | bytes 5062664 | tf_op jit(solution)/shard_map/ppermute | solution.py:68
  12.4 2.9 %collective-permute-start = (bf16[80,512]{1,0:T(8,128)(2,1)S(1)}, bf16[80,512]{1,0:T(8,128)(2,1)S(1)}, u32[]{:S(2)}, u32[]{:S(2)}) collective-permute-start(bf16[80,512]{1,0:T(8,128)(2,1)S(1)} %get-tuple-element.44), channel_id=1, source_target_pairs={{0,8},{8,0},{1,9},{9,1},{2,10},{10,2},{3,11},{11,3},{4,12},{12,4},... | collective-permute-start | bytes 245768 | tf_op jit(solution)/shard_map/ppermute | solution.py:68
  15.2 6.6 %collective-permute-start.1 = (bf16[80,1024]{1,0:T(8,128)(2,1)S(1)}, bf16[80,1024]{1,0:T(8,128)(2,1)S(1)}, u32[]{:S(2)}, u32[]{:S(2)}) collective-permute-start(bf16[80,1024]{1,0:T(8,128)(2,1)S(1)} %shard_map.114.a), channel_id=1, source_target_pairs={{0,4},{4,0},{1,5},{5,1},{2,6},{6,2},{3,7},{7,3},{8,12},{12,8},{9,1... | collective-permute-start | bytes 491528 | tf_op jit(solution)/shard_map/ppermute | solution.py:68
  21.8 11.9 %collective-permute-start.2 = (bf16[2,80,1024]{2,1,0:T(8,128)(2,1)S(1)}, bf16[2,80,1024]{2,1,0:T(8,128)(2,1)S(1)}, u32[]{:S(2)}, u32[]{:S(2)}) collective-permute-start(bf16[2,80,1024]{2,1,0:T(8,128)(2,1)S(1)} %shard_map.115.g0), channel_id=1, source_target_pairs={{0,1},{1,2},{2,3},{3,0},{4,5},{5,6},{6,7},{7,4},{8,9},{9,10},{10,1... | collective-permute-start | bytes 983048 | tf_op jit(solution)/shard_map/ppermute | solution.py:72
  23.9 17.7 %collective-permute-start.3 = (bf16[2,80,1024]{2,1,0:T(8,128)(2,1)S(1)}, bf16[2,80,1024]{2,1,0:T(8,128)(2,1)S(1)}, u32[]{:S(2)}, u32[]{:S(2)}) collective-permute-start(bf16[2,80,1024]{2,1,0:T(8,128)(2,1)S(1)} %shard_map.115.g0), channel_id=1, source_target_pairs={{0,2},{1,3},{2,0},{3,1},{4,6},{5,7},{6,4},{7,5},{8,10},{9,11},{10,... | collective-permute-start | bytes 983048 | tf_op jit(solution)/shard_map/ppermute | solution.py:72
  27.5 14.1 %collective-permute-start.4 = (bf16[2,80,1024]{2,1,0:T(8,128)(2,1)S(1)}, bf16[2,80,1024]{2,1,0:T(8,128)(2,1)S(1)}, u32[]{:S(2)}, u32[]{:S(2)}) collective-permute-start(bf16[2,80,1024]{2,1,0:T(8,128)(2,1)S(1)} %shard_map.115.g0), channel_id=1, source_target_pairs={{0,3},{1,0},{2,1},{3,2},{4,7},{5,4},{6,5},{7,6},{8,11},{9,8},{10,9... | collective-permute-start | bytes 983048 | tf_op jit(solution)/shard_map/ppermute | solution.py:72
  46.9 38.0 %collective-permute-start.7 = (bf16[4,32,3696]{2,1,0:T(8,128)(2,1)S(1)}, bf16[4,32,3696]{2,1,0:T(8,128)(2,1)S(1)}, u32[]{:S(2)}, u32[]{:S(2)}) collective-permute-start(bf16[4,32,3696]{2,1,0:T(8,128)(2,1)S(1)} %get-tuple-element.46), channel_id=1, source_target_pairs={{0,16},{16,0},{1,17},{17,1},{2,18},{18,2},{3,19},{19,3},{4,20},{20... | collective-permute-start | bytes 2838536 | tf_op jit(solution)/shard_map/ppermute | solution.py:68
  55.0 161.3 %copy-start = (bf16[3696,512]{1,0:T(8,128)(2,1)}, bf16[3696,512]{1,0:T(8,128)(2,1)S(1)}, u32[]{:S(2)}) copy-start(bf16[3696,512]{1,0:T(8,128)(2,1)S(1)} %shard_map.125.refs_6_.refs_4_.refs_2_) | copy-start | bytes 11354116
  55.0 141.7 %collective-permute-start.28 = (bf16[3696,512]{1,0:T(8,128)(2,1)S(1)}, bf16[3696,512]{1,0:T(8,128)(2,1)S(1)}, u32[]{:S(2)}, u32[]{:S(2)}) collective-permute-start(bf16[3696,512]{1,0:T(8,128)(2,1)S(1)} %shard_map.125.refs_6_.refs_4_.refs_2_), channel_id=1, source_target_pairs={{0,8},{8,0},{1,9},{9,1},{2,10},{10,2},{3,11},{11,3},{4,12},{12,4},... | collective-permute-start | bytes 11354120 | tf_op jit(solution)/shard_map/ppermute | solution.py:68
  60.0 156.3 %copy-start.2 = (bf16[3696,512]{1,0:T(8,128)(2,1)}, bf16[3696,512]{1,0:T(8,128)(2,1)S(1)}, u32[]{:S(2)}) copy-start(bf16[3696,512]{1,0:T(8,128)(2,1)S(1)} %shard_map.126.refs_7_.refs_5_.refs_3_) | copy-start | bytes 11354116
  60.0 137.1 %collective-permute-start.29 = (bf16[3696,512]{1,0:T(8,128)(2,1)S(1)}, bf16[3696,512]{1,0:T(8,128)(2,1)S(1)}, u32[]{:S(2)}, u32[]{:S(2)}) collective-permute-start(bf16[3696,512]{1,0:T(8,128)(2,1)S(1)} %shard_map.126.refs_7_.refs_5_.refs_3_), channel_id=1, source_target_pairs={{0,8},{8,0},{1,9},{9,1},{2,10},{10,2},{3,11},{11,3},{4,12},{12,4},... | collective-permute-start | bytes 11354120 | tf_op jit(solution)/shard_map/ppermute | solution.py:68
  60.6 11.5 %collective-permute-start.12 = (bf16[48,3696]{1,0:T(8,128)(2,1)S(1)}, bf16[48,3696]{1,0:T(8,128)(2,1)S(1)}, u32[]{:S(2)}, u32[]{:S(2)}) collective-permute-start(bf16[48,3696]{1,0:T(8,128)(2,1)S(1)} %get-tuple-element.53), channel_id=1, source_target_pairs={{0,32},{32,64},{64,96},{96,0},{1,33},{33,65},{65,97},{97,1},{2,34}... | collective-permute-start | bytes 1064456 | tf_op jit(solution)/shard_map/ppermute | solution.py:64
  62.1 10.3 %collective-permute-start.13 = (bf16[48,3696]{1,0:T(8,128)(2,1)S(1)}, bf16[48,3696]{1,0:T(8,128)(2,1)S(1)}, u32[]{:S(2)}, u32[]{:S(2)}) collective-permute-start(bf16[48,3696]{1,0:T(8,128)(2,1)S(1)} %get-tuple-element.55), channel_id=1, source_target_pairs={{0,96},{32,0},{64,32},{96,64},{1,97},{33,1},{65,33},{97,65},{2,98}... | collective-permute-start | bytes 1064456 | tf_op jit(solution)/shard_map/ppermute | solution.py:64
  72.1 10.7 %collective-permute-start.15 = (bf16[48,3696]{1,0:T(8,128)(2,1)S(1)}, bf16[48,3696]{1,0:T(8,128)(2,1)S(1)}, u32[]{:S(2)}, u32[]{:S(2)}) collective-permute-start(bf16[48,3696]{1,0:T(8,128)(2,1)S(1)} %get-tuple-element.58), channel_id=1, source_target_pairs={{0,32},{32,64},{64,96},{96,0},{1,33},{33,65},{65,97},{97,1},{2,34}... | collective-permute-start | bytes 1064456 | tf_op jit(solution)/shard_map/ppermute | solution.py:64
  72.6 10.5 %collective-permute-start.16 = (bf16[48,3696]{1,0:T(8,128)(2,1)S(1)}, bf16[48,3696]{1,0:T(8,128)(2,1)S(1)}, u32[]{:S(2)}, u32[]{:S(2)}) collective-permute-start(bf16[48,3696]{1,0:T(8,128)(2,1)S(1)} %get-tuple-element.59), channel_id=1, source_target_pairs={{0,96},{32,0},{64,32},{96,64},{1,97},{33,1},{65,33},{97,65},{2,98}... | collective-permute-start | bytes 1064456 | tf_op jit(solution)/shard_map/ppermute | solution.py:64
  82.8 8.6 %collective-permute-start.11 = (bf16[48,3696]{1,0:T(8,128)(2,1)S(1)}, bf16[48,3696]{1,0:T(8,128)(2,1)S(1)}, u32[]{:S(2)}, u32[]{:S(2)}) collective-permute-start(bf16[48,3696]{1,0:T(8,128)(2,1)S(1)} %get-tuple-element.51), channel_id=1, source_target_pairs={{0,96},{32,0},{64,32},{96,64},{1,97},{33,1},{65,33},{97,65},{2,98}... | collective-permute-start | bytes 1064456 | tf_op jit(solution)/shard_map/ppermute | solution.py:64
  83.1 10.6 %collective-permute-start.14 = (bf16[48,3696]{1,0:T(8,128)(2,1)S(1)}, bf16[48,3696]{1,0:T(8,128)(2,1)S(1)}, u32[]{:S(2)}, u32[]{:S(2)}) collective-permute-start(bf16[48,3696]{1,0:T(8,128)(2,1)S(1)} %get-tuple-element.56), channel_id=1, source_target_pairs={{0,32},{32,64},{64,96},{96,0},{1,33},{33,65},{65,97},{97,1},{2,34}... | collective-permute-start | bytes 1064456 | tf_op jit(solution)/shard_map/ppermute | solution.py:64
  84.9 9.6 %collective-permute-start.17 = (bf16[48,3696]{1,0:T(8,128)(2,1)S(1)}, bf16[48,3696]{1,0:T(8,128)(2,1)S(1)}, u32[]{:S(2)}, u32[]{:S(2)}) collective-permute-start(bf16[48,3696]{1,0:T(8,128)(2,1)S(1)} %shard_map.121), channel_id=1, source_target_pairs={{0,16},{16,0},{1,17},{17,1},{2,18},{18,2},{3,19},{19,3},{4,20},{20... | collective-permute-start | bytes 1064456 | tf_op jit(solution)/shard_map/ppermute | solution.py:68
  85.4 46.1 %copy-start.17 = (f32[3]{0:T(128)S(1)}, f32[3]{0:T(128)}, u32[]{:S(2)}) copy-start(f32[3]{0:T(128)} %scale.9) | copy-start | bytes 40
  91.4 6.1 %collective-permute-start.10 = (bf16[32,3696]{1,0:T(8,128)(2,1)S(1)}, bf16[32,3696]{1,0:T(8,128)(2,1)S(1)}, u32[]{:S(2)}, u32[]{:S(2)}) collective-permute-start(bf16[32,3696]{1,0:T(8,128)(2,1)S(1)} %get-tuple-element.49), channel_id=1, source_target_pairs={{0,96},{32,0},{64,32},{96,64},{1,97},{33,1},{65,33},{97,65},{2,98}... | collective-permute-start | bytes 709640 | tf_op jit(solution)/shard_map/ppermute | solution.py:64
  93.7 39.3 %collective-permute-start.19 = (bf16[2,80,3696]{2,1,0:T(8,128)(2,1)S(1)}, bf16[2,80,3696]{2,1,0:T(8,128)(2,1)S(1)}, u32[]{:S(2)}, u32[]{:S(2)}) collective-permute-start(bf16[2,80,3696]{2,1,0:T(8,128)(2,1)S(1)} %shard_map.122), channel_id=1, source_target_pairs={{0,32},{32,64},{64,96},{96,0},{1,33},{33,65},{65,97},{97,1},{2,34}... | collective-permute-start | bytes 3548168 | tf_op jit(solution)/shard_map/ppermute | solution.py:64
  94.6 36.6 %collective-permute-start.8 = (bf16[32,3696]{1,0:T(8,128)(2,1)S(1)}, bf16[32,3696]{1,0:T(8,128)(2,1)S(1)}, u32[]{:S(2)}, u32[]{:S(2)}) collective-permute-start(bf16[32,3696]{1,0:T(8,128)(2,1)S(1)} %get-tuple-element.47), channel_id=1, source_target_pairs={{0,32},{32,64},{64,96},{96,0},{1,33},{33,65},{65,97},{97,1},{2,34}... | collective-permute-start | bytes 709640 | tf_op jit(solution)/shard_map/ppermute | solution.py:64
  97.5 33.7 %collective-permute-start.9 = (bf16[32,3696]{1,0:T(8,128)(2,1)S(1)}, bf16[32,3696]{1,0:T(8,128)(2,1)S(1)}, u32[]{:S(2)}, u32[]{:S(2)}) collective-permute-start(bf16[32,3696]{1,0:T(8,128)(2,1)S(1)} %get-tuple-element.48), channel_id=1, source_target_pairs={{0,64},{32,96},{64,0},{96,32},{1,65},{33,97},{65,1},{97,33},{2,66}... | collective-permute-start | bytes 709640 | tf_op jit(solution)/shard_map/ppermute | solution.py:64
  131.1 21.7 %collective-permute-start.21 = (bf16[2,80,3696]{2,1,0:T(8,128)(2,1)S(1)}, bf16[2,80,3696]{2,1,0:T(8,128)(2,1)S(1)}, u32[]{:S(2)}, u32[]{:S(2)}) collective-permute-start(bf16[2,80,3696]{2,1,0:T(8,128)(2,1)S(1)} %shard_map.122), channel_id=1, source_target_pairs={{0,96},{32,0},{64,32},{96,64},{1,97},{33,1},{65,33},{97,65},{2,98}... | collective-permute-start | bytes 3548168 | tf_op jit(solution)/shard_map/ppermute | solution.py:64
  131.1 30.5 %collective-permute-start.23 = (bf16[2,80,3696]{2,1,0:T(8,128)(2,1)S(1)}, bf16[2,80,3696]{2,1,0:T(8,128)(2,1)S(1)}, u32[]{:S(2)}, u32[]{:S(2)}) collective-permute-start(bf16[2,80,3696]{2,1,0:T(8,128)(2,1)S(1)} %shard_map.122), channel_id=1, source_target_pairs={{0,16},{16,0},{1,17},{17,1},{2,18},{18,2},{3,19},{19,3},{4,20},{20... | collective-permute-start | bytes 3548168 | tf_op jit(solution)/shard_map/ppermute | solution.py:68
  133.0 32.9 %collective-permute-start.25 = (bf16[48,3696]{1,0:T(8,128)(2,1)S(1)}, bf16[48,3696]{1,0:T(8,128)(2,1)S(1)}, u32[]{:S(2)}, u32[]{:S(2)}) collective-permute-start(bf16[48,3696]{1,0:T(8,128)(2,1)S(1)} %get-tuple-element.60), channel_id=1, source_target_pairs={{0,16},{16,0},{1,17},{17,1},{2,18},{18,2},{3,19},{19,3},{4,20},{20... | collective-permute-start | bytes 1064456 | tf_op jit(solution)/shard_map/ppermute | solution.py:68
  152.9 15.6 %collective-permute-start.22 = (bf16[32,3696]{1,0:T(8,128)(2,1)S(1)}, bf16[32,3696]{1,0:T(8,128)(2,1)S(1)}, u32[]{:S(2)}, u32[]{:S(2)}) collective-permute-start(bf16[32,3696]{1,0:T(8,128)(2,1)S(1)} %get-tuple-element.61), channel_id=1, source_target_pairs={{0,16},{16,0},{1,17},{17,1},{2,18},{18,2},{3,19},{19,3},{4,20},{20... | collective-permute-start | bytes 709640 | tf_op jit(solution)/shard_map/ppermute | solution.py:68
  161.7 10.5 %collective-permute-start.18 = (bf16[48,3696]{1,0:T(8,128)(2,1)S(1)}, bf16[48,3696]{1,0:T(8,128)(2,1)S(1)}, u32[]{:S(2)}, u32[]{:S(2)}) collective-permute-start(bf16[48,3696]{1,0:T(8,128)(2,1)S(1)} %get-tuple-element.60), channel_id=1, source_target_pairs={{0,32},{32,64},{64,96},{96,0},{1,33},{33,65},{65,97},{97,1},{2,34}... | collective-permute-start | bytes 1064456 | tf_op jit(solution)/shard_map/ppermute | solution.py:64
  165.9 11.2 %collective-permute-start.20 = (bf16[48,3696]{1,0:T(8,128)(2,1)S(1)}, bf16[48,3696]{1,0:T(8,128)(2,1)S(1)}, u32[]{:S(2)}, u32[]{:S(2)}) collective-permute-start(bf16[48,3696]{1,0:T(8,128)(2,1)S(1)} %get-tuple-element.60), channel_id=1, source_target_pairs={{0,96},{32,0},{64,32},{96,64},{1,97},{33,1},{65,33},{97,65},{2,98}... | collective-permute-start | bytes 1064456 | tf_op jit(solution)/shard_map/ppermute | solution.py:64
  168.5 25.6 %collective-permute-start.26 = (bf16[2,48,3696]{2,1,0:T(8,128)(2,1)S(1)}, bf16[2,48,3696]{2,1,0:T(8,128)(2,1)S(1)}, u32[]{:S(2)}, u32[]{:S(2)}) collective-permute-start(bf16[2,48,3696]{2,1,0:T(8,128)(2,1)S(1)} %shard_map.124.refs_5_), channel_id=1, source_target_pairs={{0,96},{32,0},{64,32},{96,64},{1,97},{33,1},{65,33},{97,65},{2,98}... | collective-permute-start | bytes 2128904 | tf_op jit(solution)/shard_map/ppermute | solution.py:64
  172.1 9.9 %collective-permute-start.30 = (bf16[32,3696]{1,0:T(8,128)(2,1)S(1)}, bf16[32,3696]{1,0:T(8,128)(2,1)S(1)}, u32[]{:S(2)}, u32[]{:S(2)}) collective-permute-start(bf16[32,3696]{1,0:T(8,128)(2,1)S(1)} %get-tuple-element.61), channel_id=1, source_target_pairs={{0,32},{32,64},{64,96},{96,0},{1,33},{33,65},{65,97},{97,1},{2,34}... | collective-permute-start | bytes 709640 | tf_op jit(solution)/shard_map/ppermute | solution.py:64
  177.1 12.9 %collective-permute-start.31 = (bf16[32,3696]{1,0:T(8,128)(2,1)S(1)}, bf16[32,3696]{1,0:T(8,128)(2,1)S(1)}, u32[]{:S(2)}, u32[]{:S(2)}) collective-permute-start(bf16[32,3696]{1,0:T(8,128)(2,1)S(1)} %get-tuple-element.61), channel_id=1, source_target_pairs={{0,96},{32,0},{64,32},{96,64},{1,97},{33,1},{65,33},{97,65},{2,98}... | collective-permute-start | bytes 709640 | tf_op jit(solution)/shard_map/ppermute | solution.py:64
  182.0 22.7 %collective-permute-start.32 = (bf16[2,48,3696]{2,1,0:T(8,128)(2,1)S(1)}, bf16[2,48,3696]{2,1,0:T(8,128)(2,1)S(1)}, u32[]{:S(2)}, u32[]{:S(2)}) collective-permute-start(bf16[2,48,3696]{2,1,0:T(8,128)(2,1)S(1)} %shard_map.124.refs_5_), channel_id=1, source_target_pairs={{0,32},{32,64},{64,96},{96,0},{1,33},{33,65},{65,97},{97,1},{2,34}... | collective-permute-start | bytes 2128904 | tf_op jit(solution)/shard_map/ppermute | solution.py:64
  190.0 22.2 %collective-permute-start.24 = (bf16[2,48,3696]{2,1,0:T(8,128)(2,1)S(1)}, bf16[2,48,3696]{2,1,0:T(8,128)(2,1)S(1)}, u32[]{:S(2)}, u32[]{:S(2)}) collective-permute-start(bf16[2,48,3696]{2,1,0:T(8,128)(2,1)S(1)} %get-tuple-element.62.refs_2_), channel_id=1, source_target_pairs={{0,32},{32,64},{64,96},{96,0},{1,33},{33,65},{65,97},{97,1},{2,34}... | collective-permute-start | bytes 2128904 | tf_op jit(solution)/shard_map/ppermute | solution.py:64
  194.1 22.2 %collective-permute-start.27 = (bf16[2,48,3696]{2,1,0:T(8,128)(2,1)S(1)}, bf16[2,48,3696]{2,1,0:T(8,128)(2,1)S(1)}, u32[]{:S(2)}, u32[]{:S(2)}) collective-permute-start(bf16[2,48,3696]{2,1,0:T(8,128)(2,1)S(1)} %collective-permute-done.26.refs_1_), channel_id=1, source_target_pairs={{0,96},{32,0},{64,32},{96,64},{1,97},{33,1},{65,33},{97,65},{2,98}... | collective-permute-start | bytes 2128904 | tf_op jit(solution)/shard_map/ppermute | solution.py:64
  196.7 40.2 %collective-permute-start.35 = (bf16[2,32,3696]{2,1,0:T(8,128)(2,1)S(1)}, bf16[2,32,3696]{2,1,0:T(8,128)(2,1)S(1)}, u32[]{:S(2)}, u32[]{:S(2)}) collective-permute-start(bf16[2,32,3696]{2,1,0:T(8,128)(2,1)S(1)} %get-tuple-element.64.refs_1_), channel_id=1, source_target_pairs={{0,16},{16,0},{1,17},{17,1},{2,18},{18,2},{3,19},{19,3},{4,20},{20... | collective-permute-start | bytes 1419272 | tf_op jit(solution)/shard_map/ppermute | solution.py:68
  197.1 39.8 %collective-permute-start.36 = (bf16[2,32,3696]{2,1,0:T(8,128)(2,1)S(1)}, bf16[2,32,3696]{2,1,0:T(8,128)(2,1)S(1)}, u32[]{:S(2)}, u32[]{:S(2)}) collective-permute-start(bf16[2,32,3696]{2,1,0:T(8,128)(2,1)S(1)} %get-tuple-element.65.refs_2_), channel_id=1, source_target_pairs={{0,16},{16,0},{1,17},{17,1},{2,18},{18,2},{3,19},{19,3},{4,20},{20... | collective-permute-start | bytes 1419272 | tf_op jit(solution)/shard_map/ppermute | solution.py:68
  204.7 19.3 %collective-permute-start.33 = (bf16[32,3696]{1,0:T(8,128)(2,1)}, bf16[32,3696]{1,0:T(8,128)(2,1)S(1)}, u32[]{:S(2)}, u32[]{:S(2)}) collective-permute-start(bf16[32,3696]{1,0:T(8,128)(2,1)} %get-tuple-element.69), channel_id=1, source_target_pairs={{0,32},{32,64},{64,96},{96,0},{1,33},{33,65},{65,97},{97,1},{2,34}... | collective-permute-start | bytes 709640 | tf_op jit(solution)/shard_map/ppermute | solution.py:64
  212.2 13.7 %collective-permute-start.34 = (bf16[32,3696]{1,0:T(8,128)(2,1)}, bf16[32,3696]{1,0:T(8,128)(2,1)}, u32[]{:S(2)}, u32[]{:S(2)}) collective-permute-start(bf16[32,3696]{1,0:T(8,128)(2,1)} %get-tuple-element.70), channel_id=1, source_target_pairs={{0,96},{32,0},{64,32},{96,64},{1,97},{33,1},{65,33},{97,65},{2,98}... | collective-permute-start | bytes 709640 | tf_op jit(solution)/shard_map/ppermute | solution.py:64
  220.4 42.3 %all-to-all-start = ((bf16[8,48,1024]{2,1,0:T(8,128)(2,1)}), bf16[8,48,1024]{2,1,0:T(8,128)(2,1)S(1)}, u32[]{:S(2)}, u32[]{:S(2)}) async-start(bf16[8,48,1024]{2,1,0:T(8,128)(2,1)} %last.1), calls=%async_computation | async-start | bytes 1572864 | tf_op jit(solution)/shard_map/all_to_all | solution.py:563
  224.0 10.4 %collective-permute-start.37 = (bf16[32,3696]{1,0:T(8,128)(2,1)S(1)}, bf16[32,3696]{1,0:T(8,128)(2,1)S(1)}, u32[]{:S(2)}, u32[]{:S(2)}) collective-permute-start(bf16[32,3696]{1,0:T(8,128)(2,1)S(1)} %collective-permute-done.33.refs_0_), channel_id=1, source_target_pairs={{0,16},{16,0},{1,17},{17,1},{2,18},{18,2},{3,19},{19,3},{4,20},{20... | collective-permute-start | bytes 709640 | tf_op jit(solution)/shard_map/ppermute | solution.py:68
  225.9 11.0 %collective-permute-start.38 = (bf16[32,3696]{1,0:T(8,128)(2,1)}, bf16[32,3696]{1,0:T(8,128)(2,1)S(1)}, u32[]{:S(2)}, u32[]{:S(2)}) collective-permute-start(bf16[32,3696]{1,0:T(8,128)(2,1)} %collective-permute-done.34.refs_1_), channel_id=1, source_target_pairs={{0,16},{16,0},{1,17},{17,1},{2,18},{18,2},{3,19},{19,3},{4,20},{20... | collective-permute-start | bytes 709640 | tf_op jit(solution)/shard_map/ppermute | solution.py:68
  248.4 6.3 %collective-permute-start.39 = (bf16[2,32,1024]{2,1,0:T(8,128)(2,1)S(1)}, bf16[2,32,1024]{2,1,0:T(8,128)(2,1)S(1)}, u32[]{:S(2)}, u32[]{:S(2)}) collective-permute-start(bf16[2,32,1024]{2,1,0:T(8,128)(2,1)S(1)} %get-tuple-element.72), channel_id=1, source_target_pairs={{0,1},{1,2},{2,3},{3,0},{4,5},{5,6},{6,7},{7,4},{8,9},{9,10},{10,1... | collective-permute-start | bytes 393224 | tf_op jit(solution)/shard_map/ppermute | solution.py:72
  250.5 7.1 %collective-permute-start.40 = (bf16[2,32,1024]{2,1,0:T(8,128)(2,1)S(1)}, bf16[2,32,1024]{2,1,0:T(8,128)(2,1)S(1)}, u32[]{:S(2)}, u32[]{:S(2)}) collective-permute-start(bf16[2,32,1024]{2,1,0:T(8,128)(2,1)S(1)} %get-tuple-element.73), channel_id=1, source_target_pairs={{0,2},{1,3},{2,0},{3,1},{4,6},{5,7},{6,4},{7,5},{8,10},{9,11},{10,... | collective-permute-start | bytes 393224 | tf_op jit(solution)/shard_map/ppermute | solution.py:72
  253.3 5.0 %collective-permute-start.41 = (bf16[2,32,1024]{2,1,0:T(8,128)(2,1)S(1)}, bf16[2,32,1024]{2,1,0:T(8,128)(2,1)S(1)}, u32[]{:S(2)}, u32[]{:S(2)}) collective-permute-start(bf16[2,32,1024]{2,1,0:T(8,128)(2,1)S(1)} %get-tuple-element.74), channel_id=1, source_target_pairs={{0,3},{1,0},{2,1},{3,2},{4,7},{5,4},{6,5},{7,6},{8,11},{9,8},{10,9... | collective-permute-start | bytes 393224 | tf_op jit(solution)/shard_map/ppermute | solution.py:72
  258.3 4.3 %collective-permute-start.42 = (bf16[32,1024]{1,0:T(8,128)(2,1)S(1)}, bf16[32,1024]{1,0:T(8,128)(2,1)S(1)}, u32[]{:S(2)}, u32[]{:S(2)}) collective-permute-start(bf16[32,1024]{1,0:T(8,128)(2,1)S(1)} %get-tuple-element.76), channel_id=1, source_target_pairs={{0,4},{4,0},{1,5},{5,1},{2,6},{6,2},{3,7},{7,3},{8,12},{12,8},{9,1... | collective-permute-start | bytes 196616 | tf_op jit(solution)/shard_map/ppermute | solution.py:68
  262.9 17.2 %collective-permute-start.43 = (f32[80,512]{1,0:T(8,128)S(1)}, f32[80,512]{1,0:T(8,128)S(1)}, u32[]{:S(2)}, u32[]{:S(2)}) collective-permute-start(f32[80,512]{1,0:T(8,128)S(1)} %get-tuple-element.79), channel_id=1, source_target_pairs={{0,8},{8,0},{1,9},{9,1},{2,10},{10,2},{3,11},{11,3},{4,12},{12,4},... | collective-permute-start | bytes 491528 | tf_op jit(solution)/shard_map/ppermute | solution.py:68
  (15 other events, 150.7 us)

commit v2 on v1

--- a/solution.py
+++ b/solution.py
@@ -479,11 +479,12 @@
         for dyl in range(2):
             c = 4 * (yl ^ dyl) + (z + dz) % 4
             owners.append(2 * ((c // 2 - x) % 4) + ((c % 2) ^ yh))
-    place = jnp.stack(slots + blocks + owners + [core]).astype(jnp.int32)
-    out_grad, place = lax.optimization_barrier((out_grad, place))
-
-    def halves(place, grad, mine, theirs):
-        at = pl.multiple_of(place[24] * half, 16)
+    place = jnp.stack(slots + blocks + owners).astype(jnp.int32)
+
+    side = core.reshape(1).astype(jnp.int32)
+
+    def halves(side, grad, mine, theirs):
+        at = pl.multiple_of(side[0] * half, 16)
         mine[...] = grad[pl.ds(at, half), :]
         theirs[...] = grad[pl.ds(half - at, half), :]
 
@@ -496,8 +497,9 @@
         out[1] = b[...]
 
     rows = (half, out_grad.shape[1])
-    mine, theirs = call(halves, [place, out_grad], [(rows, BF16)] * 2, smem=1)
+    mine, theirs = call(halves, [side, out_grad], [(rows, BF16)] * 2, smem=1)
     theirs = flip(theirs, "core")
+    theirs, place = lax.optimization_barrier((theirs, place))
     (acts,) = call(stacked, [gate_act, up_act], [((2, *gate_act.shape), BF16)])
     (block,) = call(beside, [mine, theirs], [((half, 2 * rows[1]), BF16)])
     block_y = flip(block, "yl")
@@ -578,16 +580,16 @@
     got = flip(other, "core")
     largest = lax.all_to_all(largest, EVERY, 0, 0, tiled=True)
 
-    def scale_up(place, largest, kept, got, grad_unit, grad_amax):
+    def scale_up(side, largest, kept, got, grad_unit, grad_amax):
         top = jnp.max(largest[...])
-        at = pl.multiple_of(place[24] * half, 16)
+        at = pl.multiple_of(side[0] * half, 16)
         grad_unit[pl.ds(at, half), :] = (6.0 * kept[...] / (top + 1e-06)).astype(BF16)
         grad_unit[pl.ds(half - at, half), :] = (6.0 * got[...] / (top + 1e-06)).astype(BF16)
         grad_amax[0] = top
 
     return call(
         scale_up,
-        [place, largest, kept, got],
+        [side, largest, kept, got],
         [((2 * half, width), BF16), ((1,), F32)],
         smem=1,
         out_specs=[VMEM, SMEM],

time: 283 us -> 282 us (level)
  transfers between devices with their start and end apart: 45 -> 45, of which waited for: 25 -> 25; matrix products, arithmetic and copies ran while one was open for 0% -> 0% of each run, Pallas kernels for 15% -> 14%
where the time goes in v2:
time: 282 us; the launch traced here: 281 us
  waiting for transfers between devices  141 us (50%)
  starting transfers between devices  59.1 us (21%)
  Pallas kernels  50 us (18%)
  blocking collectives  17.1 us (6%)
  local copies, waits for them, and re-layouts  11.5 us (4%)
    ppermute x21, waiting for transfers between devices, turn(): return lax.ppermute(a, 'x', [(i, (i + k) % 4) for i in range(4)])  89.8 us
    ppermute x17, waiting for transfers between devices, flip(): return lax.ppermute(a, axis, [(0, 1), (1, 0)])  34.6 us
    pallas_call x15, Pallas kernels, call(): pl.pallas_call(body, in_specs=[SMEM] * smem + [VMEM] * (len(args) - smem)...  32.3 us
    ppermute x21, starting transfers between devices, turn(): return lax.ppermute(a, 'x', [(i, (i + k) % 4) for i in range(4)])  23.7 us
    ppermute x17, starting transfers between devices, flip(): return lax.ppermute(a, axis, [(0, 1), (1, 0)])  18.9 us
    all_to_all x1, blocking collectives, whole(): largest = lax.all_to_all(largest, EVERY, 0, 0, tiled=True)  17.1 us
    ppermute x6, waiting for transfers between devices, turn_z(): return lax.ppermute(a, 'z', [(i, (i + k) % 4) for i in range(4)])  16.7 us
    ppermute x6, starting transfers between devices, turn_z(): return lax.ppermute(a, 'z', [(i, (i + k) % 4) for i in range(4)])  12.9 us
  transfers between devices with their start and end apart: 45, of which 25 were waited for; matrix products, arithmetic and copies ran while one was open for 0% of the time, Pallas kernels for 14%

profile of v2, /device:TPU:0, one launch (start us, length us, event | category | flops | bytes accessed | tf_op | source)
XLA Modules:
  0.0 281.2 jit_solution(8074558833621010273)
XLA Ops:
  3.7 3.4 %shard_map.116.own1 = bf16[2048,512]{1,0:T(8,128)(2,1)S(1)} custom-call(s32[1848,512]{1,0:T(8,128)S(1)} %bitcast.26, s32[231,512]{1,0:T(8,128)S(1)} %copy-done.11), custom_call_target="tpu_custom_call" | custom-call | flops 100000 | bytes 100000 | tf_op jit(solution)/shard_map/pallas_call | solution.py:52
  7.2 4.0 %shard_map.117.own2 = bf16[1648,512]{1,0:T(8,128)(2,1)} custom-call(s32[1848,512]{1,0:T(8,128)S(1)} %bitcast.27, s32[231,512]{1,0:T(8,128)S(1)} %copy-done.11), custom_call_target="tpu_custom_call" | custom-call | flops 100000 | bytes 100000 | tf_op jit(solution)/shard_map/pallas_call | solution.py:52
  12.9 2.3 collective-permute-done.b
  17.0 4.8 %collective-permute-done.1.b = bf16[80,1024]{1,0:T(8,128)(2,1)S(1)} collective-permute-done((bf16[80,1024]{1,0:T(8,128)(2,1)S(1)}, bf16[80,1024]{1,0:T(8,128)(2,1)S(1)}, u32[]{:S(2)}, u32[]{:S(2)}) %collective-permute-start.1) | collective-permute-done | bytes 163872 | tf_op jit(solution)/shard_map/ppermute | solution.py:68
  21.8 2.1 collective-permute-start.2
  23.9 3.6 %collective-permute-start.3 = (bf16[2,80,1024]{2,1,0:T(8,128)(2,1)S(1)}, bf16[2,80,1024]{2,1,0:T(8,128)(2,1)S(1)}, u32[]{:S(2)}, u32[]{:S(2)}) collective-permute-start(bf16[2,80,1024]{2,1,0:T(8,128)(2,1)S(1)} %shard_map.115.g0), channel_id=1, source_target_pairs={{0,2},{1,3},{2,0},{3,1},{4,6},{5,7},{6,4},{7,5},{8,10},{9,11},{10,... | collective-permute-start | bytes 983048 | tf_op jit(solution)/shard_map/ppermute | solution.py:72
  28.5 5.2 %collective-permute-done.2.g1 = bf16[2,80,1024]{2,1,0:T(8,128)(2,1)S(1)} collective-permute-done((bf16[2,80,1024]{2,1,0:T(8,128)(2,1)S(1)}, bf16[2,80,1024]{2,1,0:T(8,128)(2,1)S(1)}, u32[]{:S(2)}, u32[]{:S(2)}) %collective-permute-start.2) | collective-permute-done | bytes 327712 | tf_op jit(solution)/shard_map/ppermute | solution.py:72
  33.7 7.9 %collective-permute-done.3.g2 = bf16[2,80,1024]{2,1,0:T(8,128)(2,1)S(1)} collective-permute-done((bf16[2,80,1024]{2,1,0:T(8,128)(2,1)S(1)}, bf16[2,80,1024]{2,1,0:T(8,128)(2,1)S(1)}, u32[]{:S(2)}, u32[]{:S(2)}) %collective-permute-start.3) | collective-permute-done | bytes 327712 | tf_op jit(solution)/shard_map/ppermute | solution.py:72
  41.7 5.2 %shard_map.119 = (bf16[4,32,3696]{2,1,0:T(8,128)(2,1)S(1)}, bf16[48,3696]{1,0:T(8,128)(2,1)S(1)}, bf16[48,3696]{1,0:T(8,128)(2,1)S(1)}) custom-call(s32[24]{0:T(128)S(1)} %stack.99.slot.place, bf16[2,80,1024]{2,1,0:T(8,128)(2,1)S(1)} %shard_map.115.g0, bf16[2,80,1024]{2,1,0:T(8,128)(2,1)S(1)} %collective-permute-done.2.g1, ...), custom_call_target="tpu_custom_call" | custom-call | flops 100000 | bytes 100000 | tf_op jit(solution)/shard_map/pallas_call | solution.py:52
  46.9 3.3 %collective-permute-start.7 = (bf16[4,32,3696]{2,1,0:T(8,128)(2,1)S(1)}, bf16[4,32,3696]{2,1,0:T(8,128)(2,1)S(1)}, u32[]{:S(2)}, u32[]{:S(2)}) collective-permute-start(bf16[4,32,3696]{2,1,0:T(8,128)(2,1)S(1)} %get-tuple-element.46), channel_id=1, source_target_pairs={{0,16},{16,0},{1,17},{17,1},{2,18},{18,2},{3,19},{19,3},{4,20},{20... | collective-permute-start | bytes 2838536 | tf_op jit(solution)/shard_map/ppermute | solution.py:68
  50.2 4.8 %shard_map.125.refs_6_.refs_4_.refs_2_ = bf16[3696,512]{1,0:T(8,128)(2,1)S(1)} custom-call(s32[3696,256]{1,0:T(8,128)S(1)} %copy-done.9, s32[32,3696]{1,0:T(8,128)S(1)} %copy-done.14), custom_call_target="tpu_custom_call" | custom-call | flops 100000 | bytes 100000 | tf_op jit(solution)/shard_map/pallas_call | solution.py:52
  55.2 4.8 %shard_map.126.refs_7_.refs_5_.refs_3_ = bf16[3696,512]{1,0:T(8,128)(2,1)S(1)} custom-call(s32[3696,256]{1,0:T(8,128)S(1)} %copy-done.10, s32[32,3696]{1,0:T(8,128)S(1)} %copy-done.15), custom_call_target="tpu_custom_call" | custom-call | flops 100000 | bytes 100000 | tf_op jit(solution)/shard_map/pallas_call | solution.py:52
  63.8 6.2 %shard_map.118 = (bf16[4,32,3696]{2,1,0:T(8,128)(2,1)S(1)}, bf16[48,3696]{1,0:T(8,128)(2,1)S(1)}, bf16[48,3696]{1,0:T(8,128)(2,1)S(1)}, bf16[48,3696]{1,0:T(8,12...) custom-call(s32[24]{0:T(128)S(1)} %stack.99.slot.place, ...), custom_call_target="tpu_custom_call" | custom-call | flops 100000 | bytes 100000 | tf_op jit(solution)/shard_map/pallas_call | solution.py:52
  70.0 2.1 collective-permute-done.12.refs_1_
  72.6 3.0 %collective-permute-start.16 = (bf16[48,3696]{1,0:T(8,128)(2,1)S(1)}, bf16[48,3696]{1,0:T(8,128)(2,1)S(1)}, u32[]{:S(2)}, u32[]{:S(2)}) collective-permute-start(bf16[48,3696]{1,0:T(8,128)(2,1)S(1)} %get-tuple-element.59), channel_id=1, source_target_pairs={{0,96},{32,0},{64,32},{96,64},{1,97},{33,1},{65,33},{97,65},{2,98}... | collective-permute-start | bytes 1064456 | tf_op jit(solution)/shard_map/ppermute | solution.py:64
  75.6 7.2 %collective-permute-done.15.refs_1_ = bf16[48,3696]{1,0:T(8,128)(2,1)S(1)} collective-permute-done((bf16[48,3696]{1,0:T(8,128)(2,1)S(1)}, bf16[48,3696]{1,0:T(8,128)(2,1)S(1)}, u32[]{:S(2)}, u32[]{:S(2)}) %collective-permute-start.15) | collective-permute-done | bytes 354848 | tf_op jit(solution)/shard_map/ppermute | solution.py:64
  85.5 5.8 %collective-permute-done.11.r1 = bf16[48,3696]{1,0:T(8,128)(2,1)S(1)} collective-permute-done((bf16[48,3696]{1,0:T(8,128)(2,1)S(1)}, bf16[48,3696]{1,0:T(8,128)(2,1)S(1)}, u32[]{:S(2)}, u32[]{:S(2)}) %collective-permute-start.11) | collective-permute-done | bytes 354848 | tf_op jit(solution)/shard_map/ppermute | solution.py:64
  91.4 2.2 collective-permute-start.10
  94.8 2.6 collective-permute-done.10.d3
  99.2 31.9 %collective-permute-done.8.d1 = bf16[32,3696]{1,0:T(8,128)(2,1)S(1)} collective-permute-done((bf16[32,3696]{1,0:T(8,128)(2,1)S(1)}, bf16[32,3696]{1,0:T(8,128)(2,1)S(1)}, u32[]{:S(2)}, u32[]{:S(2)}) %collective-permute-start.8) | collective-permute-done | bytes 236576 | tf_op jit(solution)/shard_map/ppermute | solution.py:64
  133.0 3.2 %collective-permute-start.25 = (bf16[48,3696]{1,0:T(8,128)(2,1)S(1)}, bf16[48,3696]{1,0:T(8,128)(2,1)S(1)}, u32[]{:S(2)}, u32[]{:S(2)}) collective-permute-start(bf16[48,3696]{1,0:T(8,128)(2,1)S(1)} %get-tuple-element.60), channel_id=1, source_target_pairs={{0,16},{16,0},{1,17},{17,1},{2,18},{18,2},{3,19},{19,3},{4,20},{20... | collective-permute-start | bytes 1064456 | tf_op jit(solution)/shard_map/ppermute | solution.py:68
  136.2 16.6 %collective-permute-done.21.refs_3_ = bf16[2,80,3696]{2,1,0:T(8,128)(2,1)S(1)} collective-permute-done((bf16[2,80,3696]{2,1,0:T(8,128)(2,1)S(1)}, bf16[2,80,3696]{2,1,0:T(8,128)(2,1)S(1)}, u32[]{:S(2)}, u32[]{:S(2)}) %collective-permute-start.21) | collective-permute-done | bytes 1182752 | tf_op jit(solution)/shard_map/ppermute | solution.py:64
  153.2 8.4 %collective-permute-done.23.refs_5_.refs_1_ = bf16[2,80,3696]{2,1,0:T(8,128)(2,1)S(1)} collective-permute-done((bf16[2,80,3696]{2,1,0:T(8,128)(2,1)S(1)}, bf16[2,80,3696]{2,1,0:T(8,128)(2,1)S(1)}, u32[]{:S(2)}, u32[]{:S(2)}) %collective-permute-start.23) | collective-permute-done | bytes 1182752 | tf_op jit(solution)/shard_map/ppermute | solution.py:68
  162.5 3.5 %collective-permute-done.25.refs_0_ = bf16[48,3696]{1,0:T(8,128)(2,1)S(1)} collective-permute-done((bf16[48,3696]{1,0:T(8,128)(2,1)S(1)}, bf16[48,3696]{1,0:T(8,128)(2,1)S(1)}, u32[]{:S(2)}, u32[]{:S(2)}) %collective-permute-start.25) | collective-permute-done | bytes 354848 | tf_op jit(solution)/shard_map/ppermute | solution.py:68
  166.4 2.1 collective-permute-done.22.refs_4_
  169.6 2.6 collective-permute-done.18.refs_0_
  172.4 4.7 %collective-permute-done.20.refs_2_ = bf16[48,3696]{1,0:T(8,128)(2,1)S(1)} collective-permute-done((bf16[48,3696]{1,0:T(8,128)(2,1)S(1)}, bf16[48,3696]{1,0:T(8,128)(2,1)S(1)}, u32[]{:S(2)}, u32[]{:S(2)}) %collective-permute-start.20) | collective-permute-done | bytes 354848 | tf_op jit(solution)/shard_map/ppermute | solution.py:64
  179.3 2.6 collective-permute-done.30.refs_0_
  182.0 8.0 %collective-permute-done.31.refs_2_ = bf16[32,3696]{1,0:T(8,128)(2,1)S(1)} collective-permute-done((bf16[32,3696]{1,0:T(8,128)(2,1)S(1)}, bf16[32,3696]{1,0:T(8,128)(2,1)S(1)}, u32[]{:S(2)}, u32[]{:S(2)}) %collective-permute-start.31) | collective-permute-done | bytes 236576 | tf_op jit(solution)/shard_map/ppermute | solution.py:64
  190.0 4.1 %collective-permute-start.24 = (bf16[2,48,3696]{2,1,0:T(8,128)(2,1)S(1)}, bf16[2,48,3696]{2,1,0:T(8,128)(2,1)S(1)}, u32[]{:S(2)}, u32[]{:S(2)}) collective-permute-start(bf16[2,48,3696]{2,1,0:T(8,128)(2,1)S(1)} %get-tuple-element.62.refs_2_), channel_id=1, source_target_pairs={{0,32},{32,64},{64,96},{96,0},{1,33},{33,65},{65,97},{97,1},{2,34}... | collective-permute-start | bytes 2128904 | tf_op jit(solution)/shard_map/ppermute | solution.py:64
  197.1 3.1 %collective-permute-start.36 = (bf16[2,32,3696]{2,1,0:T(8,128)(2,1)S(1)}, bf16[2,32,3696]{2,1,0:T(8,128)(2,1)S(1)}, u32[]{:S(2)}, u32[]{:S(2)}) collective-permute-start(bf16[2,32,3696]{2,1,0:T(8,128)(2,1)S(1)} %get-tuple-element.65.refs_2_), channel_id=1, source_target_pairs={{0,16},{16,0},{1,17},{17,1},{2,18},{18,2},{3,19},{19,3},{4,20},{20... | collective-permute-start | bytes 1419272 | tf_op jit(solution)/shard_map/ppermute | solution.py:68
  200.3 4.4 %shard_map.128.refs_6_.refs_10_ = bf16[224,1024]{1,0:T(8,128)(2,1)S(1)} custom-call(f32[3]{0:T(128)S(1)} %copy-done.17, bf16[2,32,3696]{2,1,0:T(8,128)(2,1)S(1)} %get-tuple-element.63.refs_0_, bf16[2,32,3696]{2,1,0:T(8,128)(2,1)S(1)} %get-tuple-element.64.refs_1_, bf16[2,32,3696]{2,1,0:T(8,128)(2,1)S(1)} %get-tuple-element.65.refs_2_, ...), custom_call_target="tpu_custom_call" | custom-call | flops 3391094784 | bytes 18450432 | tf_op jit(solution)/shard_map/pallas_call | solution.py:362
  206.6 5.6 %collective-permute-done.24.refs_0_ = bf16[2,48,3696]{2,1,0:T(8,128)(2,1)S(1)} collective-permute-done((bf16[2,48,3696]{2,1,0:T(8,128)(2,1)S(1)}, bf16[2,48,3696]{2,1,0:T(8,128)(2,1)S(1)}, u32[]{:S(2)}, u32[]{:S(2)}) %collective-permute-start.24) | collective-permute-done | bytes 709664 | tf_op jit(solution)/shard_map/ppermute | solution.py:64
  212.2 4.1 %shard_map.129.refs_7_ = bf16[192,1024]{1,0:T(8,128)(2,1)S(1)} custom-call(f32[3]{0:T(128)S(1)} %copy-done.17, bf16[2,48,3696]{2,1,0:T(8,128)(2,1)S(1)} %get-tuple-element.68.refs_0_, bf16[2,48,3696]{2,1,0:T(8,128)(2,1)S(1)} %collective-permute-done.26.refs_1_, bf16[2,48,3696]{2,1,0:T(8,128)(2,1)S(1)} %get-tuple-element.62.refs_2_, ...), custom_call_target="tpu_custom_call" | custom-call | flops 2906652672 | bytes 17977344 | tf_op jit(solution)/shard_map/pallas_call | solution.py:362
  216.3 4.0 %last.1 = bf16[8,48,1024]{2,1,0:T(8,128)(2,1)} custom-call(f32[3]{0:T(128)S(1)} %copy-done.17, s32[24]{0:T(128)S(1)} %stack.99.slot.place, bf16[2,48,3696]{2,1,0:T(8,128)(2,1)S(1)} %collective-permute-done.24.refs_0_, bf16[2,48,3696]{2,1,0:T(8,128)(2,1)S(1)} %collective-permute-done.27.refs_1_, bf16[3696,512]{1,0:T(8,128)(2,1)S(1)} %shard_map.125.refs_6_.refs_4_.refs_2_, ...), custom_call_target="tpu_custom_call" | custom-call | flops 1453326336 | bytes 16558080 | tf_op jit(solution)/shard_map/last/pallas_call | solution.py:444
  220.4 3.6 %all-to-all-start = ((bf16[8,48,1024]{2,1,0:T(8,128)(2,1)}), bf16[8,48,1024]{2,1,0:T(8,128)(2,1)S(1)}, u32[]{:S(2)}, u32[]{:S(2)}) async-start(bf16[8,48,1024]{2,1,0:T(8,128)(2,1)} %last.1), calls=%async_computation | async-start | bytes 1572864 | tf_op jit(solution)/shard_map/all_to_all | solution.py:565
  227.6 6.8 %collective-permute-done.37.refs_4_ = bf16[32,3696]{1,0:T(8,128)(2,1)S(1)} collective-permute-done((bf16[32,3696]{1,0:T(8,128)(2,1)S(1)}, bf16[32,3696]{1,0:T(8,128)(2,1)S(1)}, u32[]{:S(2)}, u32[]{:S(2)}) %collective-permute-start.37) | collective-permute-done | bytes 236576 | tf_op jit(solution)/shard_map/ppermute | solution.py:68
  234.4 2.5 collective-permute-done.38.refs_5_
  237.0 2.1 copy-done.1
  239.0 2.1 copy-done.3
  241.1 2.1 copy-done.5
  243.2 2.1 copy-done.7
  245.2 3.2 %near_last.1 = (bf16[2,32,1024]{2,1,0:T(8,128)(2,1)S(1)}, bf16[2,32,1024]{2,1,0:T(8,128)(2,1)S(1)}, bf16[2,32,1024]{2,1,0:T(8,128)(2,1)S(1)}, bf16[2,32,1024]{2,1,0:T(8,128)(2,1)S(1)}) custom-call(f32[3]{0:T(128)S(1)} %copy-done.17, s32[24]{0:T(128)S(1)} %stack.99.slot.place, bf16[32,3696]{1,0:T(8,128)(2,1)S(1)} %collective-permute-done.33.refs_0_, ...), custom_call_target="tpu_custom_call" | custom-call | flops 1937768448 | bytes 17031168 | tf_op jit(solution)/shard_map/near_last/pallas_call | solution.py:391
  248.4 2.1 collective-permute-start.39
  250.5 2.8 collective-permute-start.40
  254.8 2.9 %collective-permute-done.40.z2 = bf16[2,32,1024]{2,1,0:T(8,128)(2,1)S(1)} collective-permute-done((bf16[2,32,1024]{2,1,0:T(8,128)(2,1)S(1)}, bf16[2,32,1024]{2,1,0:T(8,128)(2,1)S(1)}, u32[]{:S(2)}, u32[]{:S(2)}) %collective-permute-start.40) | collective-permute-done | bytes 131104 | tf_op jit(solution)/shard_map/ppermute | solution.py:72
  259.3 3.4 %collective-permute-done.42.near = bf16[32,1024]{1,0:T(8,128)(2,1)S(1)} collective-permute-done((bf16[32,1024]{1,0:T(8,128)(2,1)S(1)}, bf16[32,1024]{1,0:T(8,128)(2,1)S(1)}, u32[]{:S(2)}, u32[]{:S(2)}) %collective-permute-start.42) | collective-permute-done | bytes 65568 | tf_op jit(solution)/shard_map/ppermute | solution.py:68
  263.0 17.1 %all_to_all.10.largest = f32[128,1,128]{2,1,0:T(1,128)S(1)} all-to-all(f32[128,1,128]{2,1,0:T(1,128)S(1)} %get-tuple-element.77), channel_id=1, replica_groups=mesh['x'=4,'yh'=2,'core'=2,'yl'=2,'z'=4] {'x','yh','core','yl','z'}, dimensions={0} | all-to-all | bytes 131072 | tf_op jit(solution)/shard_map/all_to_all | solution.py:581
  (104 shorter events, 36.8 us)
Async XLA Ops:
  7.1 34.5 %collective-permute-start.5 = (bf16[2048,512]{1,0:T(8,128)(2,1)S(1)}, bf16[2048,512]{1,0:T(8,128)(2,1)}, u32[]{:S(2)}, u32[]{:S(2)}) collective-permute-start(bf16[2048,512]{1,0:T(8,128)(2,1)S(1)} %shard_map.116.own1), channel_id=1, source_target_pairs={{0,8},{8,0},{1,9},{9,1},{2,10},{10,2},{3,11},{11,3},{4,12},{12,4},... | collective-permute-start | bytes 6291464 | tf_op jit(solution)/shard_map/ppermute | solution.py:68
  11.2 30.5 %collective-permute-start.6 = (bf16[1648,512]{1,0:T(8,128)(2,1)}, bf16[1648,512]{1,0:T(8,128)(2,1)}, u32[]{:S(2)}, u32[]{:S(2)}) collective-permute-start(bf16[1648,512]{1,0:T(8,128)(2,1)} %shard_map.117.own2), channel_id=1, source_target_pairs={{0,8},{8,0},{1,9},{9,1},{2,10},{10,2},{3,11},{11,3},{4,12},{12,4},... | collective-permute-start | bytes 5062664 | tf_op jit(solution)/shard_map/ppermute | solution.py:68
  11.7 3.5 %collective-permute-start = (bf16[80,512]{1,0:T(8,128)(2,1)S(1)}, bf16[80,512]{1,0:T(8,128)(2,1)S(1)}, u32[]{:S(2)}, u32[]{:S(2)}) collective-permute-start(bf16[80,512]{1,0:T(8,128)(2,1)S(1)} %get-tuple-element.41), channel_id=1, source_target_pairs={{0,8},{8,0},{1,9},{9,1},{2,10},{10,2},{3,11},{11,3},{4,12},{12,4},... | collective-permute-start | bytes 245768 | tf_op jit(solution)/shard_map/ppermute | solution.py:68
  15.2 6.6 %collective-permute-start.1 = (bf16[80,1024]{1,0:T(8,128)(2,1)S(1)}, bf16[80,1024]{1,0:T(8,128)(2,1)S(1)}, u32[]{:S(2)}, u32[]{:S(2)}) collective-permute-start(bf16[80,1024]{1,0:T(8,128)(2,1)S(1)} %shard_map.114.a), channel_id=1, source_target_pairs={{0,4},{4,0},{1,5},{5,1},{2,6},{6,2},{3,7},{7,3},{8,12},{12,8},{9,1... | collective-permute-start | bytes 491528 | tf_op jit(solution)/shard_map/ppermute | solution.py:68
  21.8 11.9 %collective-permute-start.2 = (bf16[2,80,1024]{2,1,0:T(8,128)(2,1)S(1)}, bf16[2,80,1024]{2,1,0:T(8,128)(2,1)S(1)}, u32[]{:S(2)}, u32[]{:S(2)}) collective-permute-start(bf16[2,80,1024]{2,1,0:T(8,128)(2,1)S(1)} %shard_map.115.g0), channel_id=1, source_target_pairs={{0,1},{1,2},{2,3},{3,0},{4,5},{5,6},{6,7},{7,4},{8,9},{9,10},{10,1... | collective-permute-start | bytes 983048 | tf_op jit(solution)/shard_map/ppermute | solution.py:72
  23.9 17.7 %collective-permute-start.3 = (bf16[2,80,1024]{2,1,0:T(8,128)(2,1)S(1)}, bf16[2,80,1024]{2,1,0:T(8,128)(2,1)S(1)}, u32[]{:S(2)}, u32[]{:S(2)}) collective-permute-start(bf16[2,80,1024]{2,1,0:T(8,128)(2,1)S(1)} %shard_map.115.g0), channel_id=1, source_target_pairs={{0,2},{1,3},{2,0},{3,1},{4,6},{5,7},{6,4},{7,5},{8,10},{9,11},{10,... | collective-permute-start | bytes 983048 | tf_op jit(solution)/shard_map/ppermute | solution.py:72
  27.5 14.1 %collective-permute-start.4 = (bf16[2,80,1024]{2,1,0:T(8,128)(2,1)S(1)}, bf16[2,80,1024]{2,1,0:T(8,128)(2,1)S(1)}, u32[]{:S(2)}, u32[]{:S(2)}) collective-permute-start(bf16[2,80,1024]{2,1,0:T(8,128)(2,1)S(1)} %shard_map.115.g0), channel_id=1, source_target_pairs={{0,3},{1,0},{2,1},{3,2},{4,7},{5,4},{6,5},{7,6},{8,11},{9,8},{10,9... | collective-permute-start | bytes 983048 | tf_op jit(solution)/shard_map/ppermute | solution.py:72
  46.9 38.0 %collective-permute-start.7 = (bf16[4,32,3696]{2,1,0:T(8,128)(2,1)S(1)}, bf16[4,32,3696]{2,1,0:T(8,128)(2,1)S(1)}, u32[]{:S(2)}, u32[]{:S(2)}) collective-permute-start(bf16[4,32,3696]{2,1,0:T(8,128)(2,1)S(1)} %get-tuple-element.46), channel_id=1, source_target_pairs={{0,16},{16,0},{1,17},{17,1},{2,18},{18,2},{3,19},{19,3},{4,20},{20... | collective-permute-start | bytes 2838536 | tf_op jit(solution)/shard_map/ppermute | solution.py:68
  55.0 161.3 %copy-start = (bf16[3696,512]{1,0:T(8,128)(2,1)}, bf16[3696,512]{1,0:T(8,128)(2,1)S(1)}, u32[]{:S(2)}) copy-start(bf16[3696,512]{1,0:T(8,128)(2,1)S(1)} %shard_map.125.refs_6_.refs_4_.refs_2_) | copy-start | bytes 11354116
  55.0 141.7 %collective-permute-start.28 = (bf16[3696,512]{1,0:T(8,128)(2,1)S(1)}, bf16[3696,512]{1,0:T(8,128)(2,1)S(1)}, u32[]{:S(2)}, u32[]{:S(2)}) collective-permute-start(bf16[3696,512]{1,0:T(8,128)(2,1)S(1)} %shard_map.125.refs_6_.refs_4_.refs_2_), channel_id=1, source_target_pairs={{0,8},{8,0},{1,9},{9,1},{2,10},{10,2},{3,11},{11,3},{4,12},{12,4},... | collective-permute-start | bytes 11354120 | tf_op jit(solution)/shard_map/ppermute | solution.py:68
  60.0 156.3 %copy-start.2 = (bf16[3696,512]{1,0:T(8,128)(2,1)}, bf16[3696,512]{1,0:T(8,128)(2,1)S(1)}, u32[]{:S(2)}) copy-start(bf16[3696,512]{1,0:T(8,128)(2,1)S(1)} %shard_map.126.refs_7_.refs_5_.refs_3_) | copy-start | bytes 11354116
  60.0 137.1 %collective-permute-start.29 = (bf16[3696,512]{1,0:T(8,128)(2,1)S(1)}, bf16[3696,512]{1,0:T(8,128)(2,1)S(1)}, u32[]{:S(2)}, u32[]{:S(2)}) collective-permute-start(bf16[3696,512]{1,0:T(8,128)(2,1)S(1)} %shard_map.126.refs_7_.refs_5_.refs_3_), channel_id=1, source_target_pairs={{0,8},{8,0},{1,9},{9,1},{2,10},{10,2},{3,11},{11,3},{4,12},{12,4},... | collective-permute-start | bytes 11354120 | tf_op jit(solution)/shard_map/ppermute | solution.py:68
  60.6 11.5 %collective-permute-start.12 = (bf16[48,3696]{1,0:T(8,128)(2,1)S(1)}, bf16[48,3696]{1,0:T(8,128)(2,1)S(1)}, u32[]{:S(2)}, u32[]{:S(2)}) collective-permute-start(bf16[48,3696]{1,0:T(8,128)(2,1)S(1)} %get-tuple-element.53), channel_id=1, source_target_pairs={{0,32},{32,64},{64,96},{96,0},{1,33},{33,65},{65,97},{97,1},{2,34}... | collective-permute-start | bytes 1064456 | tf_op jit(solution)/shard_map/ppermute | solution.py:64
  62.1 10.3 %collective-permute-start.13 = (bf16[48,3696]{1,0:T(8,128)(2,1)S(1)}, bf16[48,3696]{1,0:T(8,128)(2,1)S(1)}, u32[]{:S(2)}, u32[]{:S(2)}) collective-permute-start(bf16[48,3696]{1,0:T(8,128)(2,1)S(1)} %get-tuple-element.55), channel_id=1, source_target_pairs={{0,96},{32,0},{64,32},{96,64},{1,97},{33,1},{65,33},{97,65},{2,98}... | collective-permute-start | bytes 1064456 | tf_op jit(solution)/shard_map/ppermute | solution.py:64
  72.1 10.7 %collective-permute-start.15 = (bf16[48,3696]{1,0:T(8,128)(2,1)S(1)}, bf16[48,3696]{1,0:T(8,128)(2,1)S(1)}, u32[]{:S(2)}, u32[]{:S(2)}) collective-permute-start(bf16[48,3696]{1,0:T(8,128)(2,1)S(1)} %get-tuple-element.58), channel_id=1, source_target_pairs={{0,32},{32,64},{64,96},{96,0},{1,33},{33,65},{65,97},{97,1},{2,34}... | collective-permute-start | bytes 1064456 | tf_op jit(solution)/shard_map/ppermute | solution.py:64
  72.6 10.5 %collective-permute-start.16 = (bf16[48,3696]{1,0:T(8,128)(2,1)S(1)}, bf16[48,3696]{1,0:T(8,128)(2,1)S(1)}, u32[]{:S(2)}, u32[]{:S(2)}) collective-permute-start(bf16[48,3696]{1,0:T(8,128)(2,1)S(1)} %get-tuple-element.59), channel_id=1, source_target_pairs={{0,96},{32,0},{64,32},{96,64},{1,97},{33,1},{65,33},{97,65},{2,98}... | collective-permute-start | bytes 1064456 | tf_op jit(solution)/shard_map/ppermute | solution.py:64
  82.8 8.6 %collective-permute-start.11 = (bf16[48,3696]{1,0:T(8,128)(2,1)S(1)}, bf16[48,3696]{1,0:T(8,128)(2,1)S(1)}, u32[]{:S(2)}, u32[]{:S(2)}) collective-permute-start(bf16[48,3696]{1,0:T(8,128)(2,1)S(1)} %get-tuple-element.51), channel_id=1, source_target_pairs={{0,96},{32,0},{64,32},{96,64},{1,97},{33,1},{65,33},{97,65},{2,98}... | collective-permute-start | bytes 1064456 | tf_op jit(solution)/shard_map/ppermute | solution.py:64
  83.1 10.6 %collective-permute-start.14 = (bf16[48,3696]{1,0:T(8,128)(2,1)S(1)}, bf16[48,3696]{1,0:T(8,128)(2,1)S(1)}, u32[]{:S(2)}, u32[]{:S(2)}) collective-permute-start(bf16[48,3696]{1,0:T(8,128)(2,1)S(1)} %get-tuple-element.56), channel_id=1, source_target_pairs={{0,32},{32,64},{64,96},{96,0},{1,33},{33,65},{65,97},{97,1},{2,34}... | collective-permute-start | bytes 1064456 | tf_op jit(solution)/shard_map/ppermute | solution.py:64
  84.9 9.6 %collective-permute-start.17 = (bf16[48,3696]{1,0:T(8,128)(2,1)S(1)}, bf16[48,3696]{1,0:T(8,128)(2,1)S(1)}, u32[]{:S(2)}, u32[]{:S(2)}) collective-permute-start(bf16[48,3696]{1,0:T(8,128)(2,1)S(1)} %shard_map.121), channel_id=1, source_target_pairs={{0,16},{16,0},{1,17},{17,1},{2,18},{18,2},{3,19},{19,3},{4,20},{20... | collective-permute-start | bytes 1064456 | tf_op jit(solution)/shard_map/ppermute | solution.py:68
  85.4 46.1 %copy-start.17 = (f32[3]{0:T(128)S(1)}, f32[3]{0:T(128)}, u32[]{:S(2)}) copy-start(f32[3]{0:T(128)} %scale.9) | copy-start | bytes 40
  91.4 6.1 %collective-permute-start.10 = (bf16[32,3696]{1,0:T(8,128)(2,1)S(1)}, bf16[32,3696]{1,0:T(8,128)(2,1)S(1)}, u32[]{:S(2)}, u32[]{:S(2)}) collective-permute-start(bf16[32,3696]{1,0:T(8,128)(2,1)S(1)} %get-tuple-element.49), channel_id=1, source_target_pairs={{0,96},{32,0},{64,32},{96,64},{1,97},{33,1},{65,33},{97,65},{2,98}... | collective-permute-start | bytes 709640 | tf_op jit(solution)/shard_map/ppermute | solution.py:64
  93.7 39.3 %collective-permute-start.19 = (bf16[2,80,3696]{2,1,0:T(8,128)(2,1)S(1)}, bf16[2,80,3696]{2,1,0:T(8,128)(2,1)S(1)}, u32[]{:S(2)}, u32[]{:S(2)}) collective-permute-start(bf16[2,80,3696]{2,1,0:T(8,128)(2,1)S(1)} %shard_map.122), channel_id=1, source_target_pairs={{0,32},{32,64},{64,96},{96,0},{1,33},{33,65},{65,97},{97,1},{2,34}... | collective-permute-start | bytes 3548168 | tf_op jit(solution)/shard_map/ppermute | solution.py:64
  94.6 36.6 %collective-permute-start.8 = (bf16[32,3696]{1,0:T(8,128)(2,1)S(1)}, bf16[32,3696]{1,0:T(8,128)(2,1)S(1)}, u32[]{:S(2)}, u32[]{:S(2)}) collective-permute-start(bf16[32,3696]{1,0:T(8,128)(2,1)S(1)} %get-tuple-element.47), channel_id=1, source_target_pairs={{0,32},{32,64},{64,96},{96,0},{1,33},{33,65},{65,97},{97,1},{2,34}... | collective-permute-start | bytes 709640 | tf_op jit(solution)/shard_map/ppermute | solution.py:64
  97.5 33.7 %collective-permute-start.9 = (bf16[32,3696]{1,0:T(8,128)(2,1)S(1)}, bf16[32,3696]{1,0:T(8,128)(2,1)S(1)}, u32[]{:S(2)}, u32[]{:S(2)}) collective-permute-start(bf16[32,3696]{1,0:T(8,128)(2,1)S(1)} %get-tuple-element.48), channel_id=1, source_target_pairs={{0,64},{32,96},{64,0},{96,32},{1,65},{33,97},{65,1},{97,33},{2,66}... | collective-permute-start | bytes 709640 | tf_op jit(solution)/shard_map/ppermute | solution.py:64
  131.1 21.7 %collective-permute-start.21 = (bf16[2,80,3696]{2,1,0:T(8,128)(2,1)S(1)}, bf16[2,80,3696]{2,1,0:T(8,128)(2,1)S(1)}, u32[]{:S(2)}, u32[]{:S(2)}) collective-permute-start(bf16[2,80,3696]{2,1,0:T(8,128)(2,1)S(1)} %shard_map.122), channel_id=1, source_target_pairs={{0,96},{32,0},{64,32},{96,64},{1,97},{33,1},{65,33},{97,65},{2,98}... | collective-permute-start | bytes 3548168 | tf_op jit(solution)/shard_map/ppermute | solution.py:64
  131.1 30.5 %collective-permute-start.23 = (bf16[2,80,3696]{2,1,0:T(8,128)(2,1)S(1)}, bf16[2,80,3696]{2,1,0:T(8,128)(2,1)S(1)}, u32[]{:S(2)}, u32[]{:S(2)}) collective-permute-start(bf16[2,80,3696]{2,1,0:T(8,128)(2,1)S(1)} %shard_map.122), channel_id=1, source_target_pairs={{0,16},{16,0},{1,17},{17,1},{2,18},{18,2},{3,19},{19,3},{4,20},{20... | collective-permute-start | bytes 3548168 | tf_op jit(solution)/shard_map/ppermute | solution.py:68
  133.0 32.9 %collective-permute-start.25 = (bf16[48,3696]{1,0:T(8,128)(2,1)S(1)}, bf16[48,3696]{1,0:T(8,128)(2,1)S(1)}, u32[]{:S(2)}, u32[]{:S(2)}) collective-permute-start(bf16[48,3696]{1,0:T(8,128)(2,1)S(1)} %get-tuple-element.60), channel_id=1, source_target_pairs={{0,16},{16,0},{1,17},{17,1},{2,18},{18,2},{3,19},{19,3},{4,20},{20... | collective-permute-start | bytes 1064456 | tf_op jit(solution)/shard_map/ppermute | solution.py:68
  152.9 15.6 %collective-permute-start.22 = (bf16[32,3696]{1,0:T(8,128)(2,1)S(1)}, bf16[32,3696]{1,0:T(8,128)(2,1)S(1)}, u32[]{:S(2)}, u32[]{:S(2)}) collective-permute-start(bf16[32,3696]{1,0:T(8,128)(2,1)S(1)} %get-tuple-element.61), channel_id=1, source_target_pairs={{0,16},{16,0},{1,17},{17,1},{2,18},{18,2},{3,19},{19,3},{4,20},{20... | collective-permute-start | bytes 709640 | tf_op jit(solution)/shard_map/ppermute | solution.py:68
  161.7 10.5 %collective-permute-start.18 = (bf16[48,3696]{1,0:T(8,128)(2,1)S(1)}, bf16[48,3696]{1,0:T(8,128)(2,1)S(1)}, u32[]{:S(2)}, u32[]{:S(2)}) collective-permute-start(bf16[48,3696]{1,0:T(8,128)(2,1)S(1)} %get-tuple-element.60), channel_id=1, source_target_pairs={{0,32},{32,64},{64,96},{96,0},{1,33},{33,65},{65,97},{97,1},{2,34}... | collective-permute-start | bytes 1064456 | tf_op jit(solution)/shard_map/ppermute | solution.py:64
  165.9 11.2 %collective-permute-start.20 = (bf16[48,3696]{1,0:T(8,128)(2,1)S(1)}, bf16[48,3696]{1,0:T(8,128)(2,1)S(1)}, u32[]{:S(2)}, u32[]{:S(2)}) collective-permute-start(bf16[48,3696]{1,0:T(8,128)(2,1)S(1)} %get-tuple-element.60), channel_id=1, source_target_pairs={{0,96},{32,0},{64,32},{96,64},{1,97},{33,1},{65,33},{97,65},{2,98}... | collective-permute-start | bytes 1064456 | tf_op jit(solution)/shard_map/ppermute | solution.py:64
  168.5 25.6 %collective-permute-start.26 = (bf16[2,48,3696]{2,1,0:T(8,128)(2,1)S(1)}, bf16[2,48,3696]{2,1,0:T(8,128)(2,1)S(1)}, u32[]{:S(2)}, u32[]{:S(2)}) collective-permute-start(bf16[2,48,3696]{2,1,0:T(8,128)(2,1)S(1)} %shard_map.124.refs_5_), channel_id=1, source_target_pairs={{0,96},{32,0},{64,32},{96,64},{1,97},{33,1},{65,33},{97,65},{2,98}... | collective-permute-start | bytes 2128904 | tf_op jit(solution)/shard_map/ppermute | solution.py:64
  172.1 9.9 %collective-permute-start.30 = (bf16[32,3696]{1,0:T(8,128)(2,1)S(1)}, bf16[32,3696]{1,0:T(8,128)(2,1)S(1)}, u32[]{:S(2)}, u32[]{:S(2)}) collective-permute-start(bf16[32,3696]{1,0:T(8,128)(2,1)S(1)} %get-tuple-element.61), channel_id=1, source_target_pairs={{0,32},{32,64},{64,96},{96,0},{1,33},{33,65},{65,97},{97,1},{2,34}... | collective-permute-start | bytes 709640 | tf_op jit(solution)/shard_map/ppermute | solution.py:64
  177.1 12.9 %collective-permute-start.31 = (bf16[32,3696]{1,0:T(8,128)(2,1)S(1)}, bf16[32,3696]{1,0:T(8,128)(2,1)S(1)}, u32[]{:S(2)}, u32[]{:S(2)}) collective-permute-start(bf16[32,3696]{1,0:T(8,128)(2,1)S(1)} %get-tuple-element.61), channel_id=1, source_target_pairs={{0,96},{32,0},{64,32},{96,64},{1,97},{33,1},{65,33},{97,65},{2,98}... | collective-permute-start | bytes 709640 | tf_op jit(solution)/shard_map/ppermute | solution.py:64
  182.0 22.7 %collective-permute-start.32 = (bf16[2,48,3696]{2,1,0:T(8,128)(2,1)S(1)}, bf16[2,48,3696]{2,1,0:T(8,128)(2,1)S(1)}, u32[]{:S(2)}, u32[]{:S(2)}) collective-permute-start(bf16[2,48,3696]{2,1,0:T(8,128)(2,1)S(1)} %shard_map.124.refs_5_), channel_id=1, source_target_pairs={{0,32},{32,64},{64,96},{96,0},{1,33},{33,65},{65,97},{97,1},{2,34}... | collective-permute-start | bytes 2128904 | tf_op jit(solution)/shard_map/ppermute | solution.py:64
  190.0 22.2 %collective-permute-start.24 = (bf16[2,48,3696]{2,1,0:T(8,128)(2,1)S(1)}, bf16[2,48,3696]{2,1,0:T(8,128)(2,1)S(1)}, u32[]{:S(2)}, u32[]{:S(2)}) collective-permute-start(bf16[2,48,3696]{2,1,0:T(8,128)(2,1)S(1)} %get-tuple-element.62.refs_2_), channel_id=1, source_target_pairs={{0,32},{32,64},{64,96},{96,0},{1,33},{33,65},{65,97},{97,1},{2,34}... | collective-permute-start | bytes 2128904 | tf_op jit(solution)/shard_map/ppermute | solution.py:64
  194.1 22.2 %collective-permute-start.27 = (bf16[2,48,3696]{2,1,0:T(8,128)(2,1)S(1)}, bf16[2,48,3696]{2,1,0:T(8,128)(2,1)S(1)}, u32[]{:S(2)}, u32[]{:S(2)}) collective-permute-start(bf16[2,48,3696]{2,1,0:T(8,128)(2,1)S(1)} %collective-permute-done.26.refs_1_), channel_id=1, source_target_pairs={{0,96},{32,0},{64,32},{96,64},{1,97},{33,1},{65,33},{97,65},{2,98}... | collective-permute-start | bytes 2128904 | tf_op jit(solution)/shard_map/ppermute | solution.py:64
  196.7 40.2 %collective-permute-start.35 = (bf16[2,32,3696]{2,1,0:T(8,128)(2,1)S(1)}, bf16[2,32,3696]{2,1,0:T(8,128)(2,1)S(1)}, u32[]{:S(2)}, u32[]{:S(2)}) collective-permute-start(bf16[2,32,3696]{2,1,0:T(8,128)(2,1)S(1)} %get-tuple-element.64.refs_1_), channel_id=1, source_target_pairs={{0,16},{16,0},{1,17},{17,1},{2,18},{18,2},{3,19},{19,3},{4,20},{20... | collective-permute-start | bytes 1419272 | tf_op jit(solution)/shard_map/ppermute | solution.py:68
  197.1 39.8 %collective-permute-start.36 = (bf16[2,32,3696]{2,1,0:T(8,128)(2,1)S(1)}, bf16[2,32,3696]{2,1,0:T(8,128)(2,1)S(1)}, u32[]{:S(2)}, u32[]{:S(2)}) collective-permute-start(bf16[2,32,3696]{2,1,0:T(8,128)(2,1)S(1)} %get-tuple-element.65.refs_2_), channel_id=1, source_target_pairs={{0,16},{16,0},{1,17},{17,1},{2,18},{18,2},{3,19},{19,3},{4,20},{20... | collective-permute-start | bytes 1419272 | tf_op jit(solution)/shard_map/ppermute | solution.py:68
  204.7 19.3 %collective-permute-start.33 = (bf16[32,3696]{1,0:T(8,128)(2,1)}, bf16[32,3696]{1,0:T(8,128)(2,1)S(1)}, u32[]{:S(2)}, u32[]{:S(2)}) collective-permute-start(bf16[32,3696]{1,0:T(8,128)(2,1)} %get-tuple-element.69), channel_id=1, source_target_pairs={{0,32},{32,64},{64,96},{96,0},{1,33},{33,65},{65,97},{97,1},{2,34}... | collective-permute-start | bytes 709640 | tf_op jit(solution)/shard_map/ppermute | solution.py:64
  212.2 13.7 %collective-permute-start.34 = (bf16[32,3696]{1,0:T(8,128)(2,1)}, bf16[32,3696]{1,0:T(8,128)(2,1)}, u32[]{:S(2)}, u32[]{:S(2)}) collective-permute-start(bf16[32,3696]{1,0:T(8,128)(2,1)} %get-tuple-element.70), channel_id=1, source_target_pairs={{0,96},{32,0},{64,32},{96,64},{1,97},{33,1},{65,33},{97,65},{2,98}... | collective-permute-start | bytes 709640 | tf_op jit(solution)/shard_map/ppermute | solution.py:64
  220.4 42.3 %all-to-all-start = ((bf16[8,48,1024]{2,1,0:T(8,128)(2,1)}), bf16[8,48,1024]{2,1,0:T(8,128)(2,1)S(1)}, u32[]{:S(2)}, u32[]{:S(2)}) async-start(bf16[8,48,1024]{2,1,0:T(8,128)(2,1)} %last.1), calls=%async_computation | async-start | bytes 1572864 | tf_op jit(solution)/shard_map/all_to_all | solution.py:565
  224.0 10.4 %collective-permute-start.37 = (bf16[32,3696]{1,0:T(8,128)(2,1)S(1)}, bf16[32,3696]{1,0:T(8,128)(2,1)S(1)}, u32[]{:S(2)}, u32[]{:S(2)}) collective-permute-start(bf16[32,3696]{1,0:T(8,128)(2,1)S(1)} %collective-permute-done.33.refs_0_), channel_id=1, source_target_pairs={{0,16},{16,0},{1,17},{17,1},{2,18},{18,2},{3,19},{19,3},{4,20},{20... | collective-permute-start | bytes 709640 | tf_op jit(solution)/shard_map/ppermute | solution.py:68
  225.9 11.0 %collective-permute-start.38 = (bf16[32,3696]{1,0:T(8,128)(2,1)}, bf16[32,3696]{1,0:T(8,128)(2,1)S(1)}, u32[]{:S(2)}, u32[]{:S(2)}) collective-permute-start(bf16[32,3696]{1,0:T(8,128)(2,1)} %collective-permute-done.34.refs_1_), channel_id=1, source_target_pairs={{0,16},{16,0},{1,17},{17,1},{2,18},{18,2},{3,19},{19,3},{4,20},{20... | collective-permute-start | bytes 709640 | tf_op jit(solution)/shard_map/ppermute | solution.py:68
  248.4 6.3 %collective-permute-start.39 = (bf16[2,32,1024]{2,1,0:T(8,128)(2,1)S(1)}, bf16[2,32,1024]{2,1,0:T(8,128)(2,1)S(1)}, u32[]{:S(2)}, u32[]{:S(2)}) collective-permute-start(bf16[2,32,1024]{2,1,0:T(8,128)(2,1)S(1)} %get-tuple-element.72), channel_id=1, source_target_pairs={{0,1},{1,2},{2,3},{3,0},{4,5},{5,6},{6,7},{7,4},{8,9},{9,10},{10,1... | collective-permute-start | bytes 393224 | tf_op jit(solution)/shard_map/ppermute | solution.py:72
  250.5 7.1 %collective-permute-start.40 = (bf16[2,32,1024]{2,1,0:T(8,128)(2,1)S(1)}, bf16[2,32,1024]{2,1,0:T(8,128)(2,1)S(1)}, u32[]{:S(2)}, u32[]{:S(2)}) collective-permute-start(bf16[2,32,1024]{2,1,0:T(8,128)(2,1)S(1)} %get-tuple-element.73), channel_id=1, source_target_pairs={{0,2},{1,3},{2,0},{3,1},{4,6},{5,7},{6,4},{7,5},{8,10},{9,11},{10,... | collective-permute-start | bytes 393224 | tf_op jit(solution)/shard_map/ppermute | solution.py:72
  253.3 5.0 %collective-permute-start.41 = (bf16[2,32,1024]{2,1,0:T(8,128)(2,1)S(1)}, bf16[2,32,1024]{2,1,0:T(8,128)(2,1)S(1)}, u32[]{:S(2)}, u32[]{:S(2)}) collective-permute-start(bf16[2,32,1024]{2,1,0:T(8,128)(2,1)S(1)} %get-tuple-element.74), channel_id=1, source_target_pairs={{0,3},{1,0},{2,1},{3,2},{4,7},{5,4},{6,5},{7,6},{8,11},{9,8},{10,9... | collective-permute-start | bytes 393224 | tf_op jit(solution)/shard_map/ppermute | solution.py:72
  258.3 4.3 %collective-permute-start.42 = (bf16[32,1024]{1,0:T(8,128)(2,1)S(1)}, bf16[32,1024]{1,0:T(8,128)(2,1)S(1)}, u32[]{:S(2)}, u32[]{:S(2)}) collective-permute-start(bf16[32,1024]{1,0:T(8,128)(2,1)S(1)} %get-tuple-element.76), channel_id=1, source_target_pairs={{0,4},{4,0},{1,5},{5,1},{2,6},{6,2},{3,7},{7,3},{8,12},{12,8},{9,1... | collective-permute-start | bytes 196616 | tf_op jit(solution)/shard_map/ppermute | solution.py:68
  262.9 17.2 %collective-permute-start.43 = (f32[80,512]{1,0:T(8,128)S(1)}, f32[80,512]{1,0:T(8,128)S(1)}, u32[]{:S(2)}, u32[]{:S(2)}) collective-permute-start(f32[80,512]{1,0:T(8,128)S(1)} %get-tuple-element.79), channel_id=1, source_target_pairs={{0,8},{8,0},{1,9},{9,1},{2,10},{10,2},{3,11},{11,3},{4,12},{12,4},... | collective-permute-start | bytes 491528 | tf_op jit(solution)/shard_map/ppermute | solution.py:68
  (15 other events, 150.6 us)
